TPU v7x, 32 devices: a whole 2x2x4 slice. The times are simulated.
32 devices in a mesh: dp: 16 (over z, x, core), tensor: 2 (over y).
Axes of the slice: x: 2, y: 2, z: 4, core: 2. Of those that a mesh axis runs over, the one named last changes fastest.
Arguments:
- x_in: bfloat16 [16, 2, 1024, 768], P(None, 'tensor', 'dp'), may hold values from -6 to 6
- cotangent: bfloat16 [16, 2, 1024, 768], P(None, 'tensor', 'dp'), may hold values from -6 to 6
- lengths: int32 [16], replicated, may hold values from 1 to 2048, 24576 in all
- dealing: int32 [16], replicated, may hold values from 0 to 15, each once
- w_qkv: float32 [768, 3, 768], P('dp', None, 'tensor'), may hold values from -0.21875 to 0.21875
- w_out: float32 [768, 768], P('dp', 'tensor'), may hold values from -1.75 to 1.75
- w_in: float32 [768, 3072], P('dp', 'tensor'), may hold values from -0.21875 to 0.21875
- w_ffo: float32 [768, 3072], P('dp', 'tensor'), may hold values from -0.109375 to 0.109375
- b_qv: float32 [2, 768], P(None, 'tensor'), may hold values from -3 to 3
- b_out: float32 [768], replicated, may hold values from -3 to 3
- b_in: float32 [3072], P('tensor'), may hold values from -3 to 3
- b_ffo: float32 [768], replicated, may hold values from -3 to 3
- ln1_gain: float32 [768], replicated, may hold values from 0.1 to 1.9
- ln1_bias: float32 [768], replicated, may hold values from -3 to 3
- ln2_gain: float32 [768], replicated, may hold values from 0.1 to 1.9
- ln2_bias: float32 [768], replicated, may hold values from -3 to 3
Outputs:
- out: bfloat16 [16, 2, 1024, 768], P(None, 'tensor', 'dp')
- grad_in: bfloat16 [16, 2, 1024, 768], P(None, 'tensor', 'dp')
- grad_w_qkv: float32 [768, 3, 768], P('dp', None, 'tensor')
- grad_w_out: float32 [768, 768], P('dp', 'tensor')
- grad_w_in: float32 [768, 3072], P('dp', 'tensor')
- grad_w_ffo: float32 [768, 3072], P('dp', 'tensor')
- grad_b_qv: float32 [2, 768], P(None, 'tensor')
- grad_b_out: float32 [768], replicated
- grad_b_in: float32 [3072], P('tensor')
- grad_b_ffo: float32 [768], replicated
- grad_ln1_gain: float32 [768], replicated
- grad_ln1_bias: float32 [768], replicated
- grad_ln2_gain: float32 [768], replicated
- grad_ln2_bias: float32 [768], replicated
Inputs may be any that keep to these rules, and one draw needn't show every extreme that they name: Slot j holds lengths[j] tokens of its sequence and padding after them; some slot is full, 2048 tokens. Sequence s goes to slot dealing[s]; every slot gets one sequence.
All inputs are finite; a program needn't handle non-finite values.
Results may differ from a plain program's by a relative error of at most 0.018.
Values may be sent and summed in bfloat16 or wider, within the bound.
A program may use at most 192 MiB of HBM per device.

v0:
```python
import jax
import jax.numpy as jnp
from jax import lax
from jax.sharding import PartitionSpec as P

HEAD_DIM = 64


def slot_owner(dealing):
    places = jnp.arange(dealing.shape[0], dtype=jnp.int32)
    matches = dealing[None, :] == places[:, None]
    return jnp.sum(jnp.where(matches, places[None, :], 0), axis=1)


def contract_last(left_side, right_side):
    return lax.dot_general(
        left_side, right_side, (((1,), (1,)), ((), ())), preferred_element_type=jnp.float32
    )


def contract_first(left_side, right_side):
    return lax.dot_general(
        left_side, right_side, (((0,), (0,)), ((), ())), preferred_element_type=jnp.float32
    )


def norm_forward(values, norm_gain, norm_shift):
    centre = jnp.mean(values, axis=-1, keepdims=True)
    centred = values - centre
    inverse = lax.rsqrt(jnp.mean(centred * centred, axis=-1, keepdims=True) + 1e-06)
    normed = centred * inverse
    return (normed * norm_gain + norm_shift, normed, inverse)


def norm_backward(upstream, normed, inverse, norm_gain):
    scaled = upstream * norm_gain
    back_rows = inverse * (
        scaled
        - jnp.mean(scaled, axis=-1, keepdims=True)
        - normed * jnp.mean(scaled * normed, axis=-1, keepdims=True)
    )
    return (back_rows, jnp.sum(upstream * normed, axis=0), jnp.sum(upstream, axis=0))


def gelu_slope(values):
    return (
        0.5 * (1.0 + lax.erf(values * 0.7071067811865476))
        + values * jnp.exp(-0.5 * values * values) * 0.3989422804014327
    )


def head_forward(query_rows, key_rows, value_rows, key_valid, block_rows, score_scale):
    outputs = []
    totals = []
    for row_start in range(0, query_rows.shape[0], block_rows):
        scores = (
            contract_last(query_rows[row_start : row_start + block_rows], key_rows) * score_scale
        )
        scores = jnp.where(key_valid[None, :], scores, -jnp.inf)
        maxima = jnp.max(scores, axis=1, keepdims=True)
        weights = jnp.exp(scores - maxima)
        summed = jnp.sum(weights, axis=1, keepdims=True)
        probs_low = (weights / summed).astype(jnp.bfloat16)
        outputs.append(jnp.dot(probs_low, value_rows, preferred_element_type=jnp.float32))
        totals.append((maxima + jnp.log(summed))[:, 0])
    return (jnp.concatenate(outputs, axis=0), jnp.concatenate(totals, axis=0))


def head_backward(
    query_rows, key_rows, value_rows, mixed_grad, log_totals, key_valid, block_rows, score_scale
):
    key_grad = jnp.zeros(key_rows.shape, jnp.float32)
    value_grad = jnp.zeros(value_rows.shape, jnp.float32)
    query_parts = []
    for row_start in range(0, query_rows.shape[0], block_rows):
        query_block = query_rows[row_start : row_start + block_rows]
        grad_block = mixed_grad[row_start : row_start + block_rows]
        scores = contract_last(query_block, key_rows) * score_scale
        scores = jnp.where(key_valid[None, :], scores, -jnp.inf)
        probs = jnp.exp(scores - log_totals[row_start : row_start + block_rows][:, None])
        prob_grad = contract_last(grad_block, value_rows)
        shared = jnp.sum(probs * prob_grad, axis=1, keepdims=True)
        score_grad = (probs * (prob_grad - shared)).astype(jnp.bfloat16)
        query_parts.append(
            jnp.dot(score_grad, key_rows, preferred_element_type=jnp.float32) * score_scale
        )
        key_grad = key_grad + contract_first(score_grad, query_block) * score_scale
        value_grad = value_grad + contract_first(probs.astype(jnp.bfloat16), grad_block)
    return (jnp.concatenate(query_parts, axis=0), key_grad, value_grad)


def per_device(
    x_in,
    cotangent,
    lengths,
    dealing,
    w_qkv,
    w_out,
    w_in,
    w_ffo,
    b_qv,
    b_out,
    b_in,
    b_ffo,
    ln1_gain,
    ln1_bias,
    ln2_gain,
    ln2_bias,
):
    owners = slot_owner(dealing)
    dealt_x, dealt_grad = (
        lax.all_to_all(
            jnp.take(x_in, owners, axis=0), "dp", split_axis=0, concat_axis=2, tiled=True
        ),
        lax.all_to_all(
            jnp.take(cotangent, owners, axis=0), "dp", split_axis=0, concat_axis=2, tiled=True
        ),
    )
    tokens_half = dealt_x[0, 0]
    output_grad = dealt_grad[0, 0].astype(jnp.float32)
    half_rows = tokens_half.shape[0]
    tensor_count = lax.axis_size("tensor")
    tensor_index = lax.axis_index("tensor")
    seq_rows = half_rows * tensor_count
    model_width = tokens_half.shape[1]
    head_width = b_qv.shape[1]
    head_count = head_width // HEAD_DIM
    ffn_width = b_in.shape[0]
    block_rows = min(512, seq_rows)
    score_scale = HEAD_DIM ** (-0.5)
    key_valid = jnp.arange(seq_rows) < lengths[lax.axis_index("dp")]
    qkv_weight, out_weight, in_weight, ffo_weight = (
        lax.all_gather(w_qkv.astype(jnp.bfloat16), "dp", axis=0, tiled=True),
        lax.all_gather(w_out.astype(jnp.bfloat16), "dp", axis=0, tiled=True),
        lax.all_gather(w_in.astype(jnp.bfloat16), "dp", axis=0, tiled=True),
        lax.all_gather(w_ffo.astype(jnp.bfloat16), "dp", axis=0, tiled=True),
    )

    def split_heads(matrix):
        return matrix.reshape(seq_rows, head_count, HEAD_DIM).transpose(1, 0, 2)

    def merge_heads(stacked):
        return stacked.transpose(1, 0, 2).reshape(seq_rows, head_width)

    tokens_full = lax.all_gather(tokens_half, "tensor", axis=0, tiled=True)
    projected = jnp.einsum(
        "ld,dce->cle", tokens_full, qkv_weight, preferred_element_type=jnp.float32
    )
    query_heads = split_heads((projected[0] + b_qv[0]).astype(jnp.bfloat16))
    key_heads = split_heads(projected[1].astype(jnp.bfloat16))
    value_heads = split_heads((projected[2] + b_qv[1]).astype(jnp.bfloat16))
    mixed_heads, log_totals = lax.map(
        lambda triple: head_forward(
            triple[0], triple[1], triple[2], key_valid, block_rows, score_scale
        ),
        (query_heads, key_heads, value_heads),
    )
    mixed_low = merge_heads(mixed_heads).astype(jnp.bfloat16)
    attn_half = lax.psum_scatter(
        contract_last(
            lax.slice_in_dim(mixed_low, 0, lax.axis_size("tensor") * half_rows, axis=0), out_weight
        ).astype(jnp.bfloat16),
        "tensor",
        scatter_dimension=0,
        tiled=True,
    ).astype(jnp.float32)
    first_norm, normed_one, inverse_one = norm_forward(
        tokens_half.astype(jnp.float32) + attn_half + b_out, ln1_gain, ln1_bias
    )
    first_full = lax.all_gather(first_norm.astype(jnp.bfloat16), "tensor", axis=0, tiled=True)
    hidden = jnp.dot(first_full, in_weight, preferred_element_type=jnp.float32) + b_in
    active = jax.nn.gelu(hidden, approximate=False).astype(jnp.bfloat16)
    ffn_half = lax.psum_scatter(
        contract_last(
            lax.slice_in_dim(active, 0, lax.axis_size("tensor") * half_rows, axis=0), ffo_weight
        ).astype(jnp.bfloat16),
        "tensor",
        scatter_dimension=0,
        tiled=True,
    ).astype(jnp.float32)
    result, normed_two, inverse_two = norm_forward(
        first_norm + ffn_half + b_ffo, ln2_gain, ln2_bias
    )
    final_grad, gain_two_grad, shift_two_grad = norm_backward(
        output_grad, normed_two, inverse_two, ln2_gain
    )
    ffo_bias_grad = jnp.sum(final_grad, axis=0)
    qkv_weight, out_weight, in_weight, ffo_weight = (
        lax.all_gather(w_qkv.astype(jnp.bfloat16), "dp", axis=0, tiled=True),
        lax.all_gather(w_out.astype(jnp.bfloat16), "dp", axis=0, tiled=True),
        lax.all_gather(w_in.astype(jnp.bfloat16), "dp", axis=0, tiled=True),
        lax.all_gather(w_ffo.astype(jnp.bfloat16), "dp", axis=0, tiled=True),
    )
    ffn_grad_full = lax.all_gather(final_grad.astype(jnp.bfloat16), "tensor", axis=0, tiled=True)
    ffo_weight_grad = contract_first(ffn_grad_full, active)
    hidden_grad = (
        jnp.dot(ffn_grad_full, ffo_weight, preferred_element_type=jnp.float32) * gelu_slope(hidden)
    ).astype(jnp.bfloat16)
    in_weight_grad = contract_first(first_full, hidden_grad)
    in_bias_grad = jnp.sum(hidden_grad.astype(jnp.float32), axis=0)
    first_grad = final_grad + lax.psum_scatter(
        contract_last(
            lax.slice_in_dim(hidden_grad, 0, lax.axis_size("tensor") * half_rows, axis=0), in_weight
        ).astype(jnp.bfloat16),
        "tensor",
        scatter_dimension=0,
        tiled=True,
    ).astype(jnp.float32)
    resid_grad, gain_one_grad, shift_one_grad = norm_backward(
        first_grad, normed_one, inverse_one, ln1_gain
    )
    out_bias_grad = jnp.sum(resid_grad, axis=0)
    attn_grad_full = lax.all_gather(resid_grad.astype(jnp.bfloat16), "tensor", axis=0, tiled=True)
    out_weight_grad = contract_first(attn_grad_full, mixed_low)
    mixed_grad = jnp.dot(attn_grad_full, out_weight, preferred_element_type=jnp.float32).astype(
        jnp.bfloat16
    )
    query_grads, key_grads, value_grads = lax.map(
        lambda bundle: head_backward(
            bundle[0],
            bundle[1],
            bundle[2],
            bundle[3],
            bundle[4],
            key_valid,
            block_rows,
            score_scale,
        ),
        (query_heads, key_heads, value_heads, split_heads(mixed_grad), log_totals),
    )
    qkv_grad = jnp.stack(
        [merge_heads(query_grads), merge_heads(key_grads), merge_heads(value_grads)]
    ).astype(jnp.bfloat16)
    qv_bias_grad = jnp.stack(
        [
            jnp.sum(qkv_grad[0].astype(jnp.float32), axis=0),
            jnp.sum(qkv_grad[2].astype(jnp.float32), axis=0),
        ]
    )
    qkv_weight_grad = jnp.einsum(
        "ld,cle->dce", tokens_full, qkv_grad, preferred_element_type=jnp.float32
    )
    rows_grad = lax.slice_in_dim(qkv_grad, 0, lax.axis_size("tensor") * half_rows, axis=1)
    input_grad = resid_grad + lax.psum_scatter(
        jnp.einsum("cle,dce->ld", rows_grad, qkv_weight, preferred_element_type=jnp.float32).astype(
            jnp.bfloat16
        ),
        "tensor",
        scatter_dimension=0,
        tiled=True,
    ).astype(jnp.float32)
    qkv_sum, out_sum, in_sum, ffo_sum = (
        lax.psum_scatter(qkv_weight_grad, "dp", scatter_dimension=0, tiled=True),
        lax.psum_scatter(out_weight_grad, "dp", scatter_dimension=0, tiled=True),
        lax.psum_scatter(in_weight_grad, "dp", scatter_dimension=0, tiled=True),
        lax.psum_scatter(ffo_weight_grad, "dp", scatter_dimension=0, tiled=True),
    )
    norm_terms = jnp.stack(
        [out_bias_grad, ffo_bias_grad, gain_one_grad, shift_one_grad, gain_two_grad, shift_two_grad]
    )
    qv_padded = lax.dynamic_update_slice_in_dim(
        jnp.zeros((2, model_width), jnp.float32), qv_bias_grad, tensor_index * head_width, 1
    )
    in_padded = lax.dynamic_update_slice_in_dim(
        jnp.zeros((ffn_width * tensor_count,), jnp.float32),
        in_bias_grad,
        tensor_index * ffn_width,
        0,
    )
    norm_sums, qv_sums, in_sums = lax.psum((norm_terms, qv_padded, in_padded), ("dp", "tensor"))
    qv_share = lax.dynamic_slice_in_dim(qv_sums, tensor_index * head_width, head_width, 1)
    in_share = lax.dynamic_slice_in_dim(in_sums, tensor_index * ffn_width, ffn_width, 0)
    back_out, back_grad = (
        lax.all_to_all(
            result.astype(jnp.bfloat16)[None, None], "dp", split_axis=2, concat_axis=0, tiled=True
        ),
        lax.all_to_all(
            input_grad.astype(jnp.bfloat16)[None, None],
            "dp",
            split_axis=2,
            concat_axis=0,
            tiled=True,
        ),
    )
    return (
        jnp.take(back_out, dealing, axis=0),
        jnp.take(back_grad, dealing, axis=0),
        qkv_sum,
        out_sum,
        in_sum,
        ffo_sum,
        qv_share,
        norm_sums[0],
        in_share,
        norm_sums[1],
        norm_sums[2],
        norm_sums[3],
        norm_sums[4],
        norm_sums[5],
    )


def solution(mesh):
    return jax.shard_map(
        per_device,
        mesh=mesh,
        in_specs=(
            P(None, "tensor", "dp", None),
            P(None, "tensor", "dp", None),
            P(),
            P(),
            P("dp", None, "tensor"),
            P("dp", "tensor"),
            P("dp", "tensor"),
            P("dp", "tensor"),
            P(None, "tensor"),
            P(),
            P("tensor"),
            P(),
            P(),
            P(),
            P(),
            P(),
        ),
        out_specs=(
            P(None, "tensor", "dp", None),
            P(None, "tensor", "dp", None),
            P("dp", None, "tensor"),
            P("dp", "tensor"),
            P("dp", "tensor"),
            P("dp", "tensor"),
            P(None, "tensor"),
            P(),
            P("tensor"),
            P(),
            P(),
            P(),
            P(),
            P(),
        ),
        check_vma=False,
    )
```

profile of v0, /device:TPU:0, one launch (start us, length us, event | category | flops | bytes accessed | tf_op | source)
XLA Modules:
  0.0 1286.8 jit_solution(3330152919851395239)
XLA Ops:
  16.4 53.0 %all_to_all.42 = bf16[16,1,64,768]{3,2,1,0:T(8,128)(2,1)} all-to-all(bf16[16,1,64,768]{3,2,1,0:T(8,128)(2,1)S(1)} %get-tuple-element.272), channel_id=1, replica_groups=mesh['dp'=16,'tensor'=2] {'dp'}, dimensions={0} | all-to-all | bytes 3145728 | tf_op jit(solution)/shard_map/all_to_all | solution.py:112
  70.2 23.6 %all_gather.30 = bf16[768,384]{1,0:T(8,128)(2,1)} all-gather(bf16[48,384]{1,0:T(8,128)(2,1)S(1)} %convert_element_type.160), channel_id=1, replica_groups=mesh['dp'=16,'tensor'=2] {'dp'}, dimensions={0}, use_global_device_ids=true | all-gather | bytes 626688 | tf_op jit(solution)/shard_map/all_gather | solution.py:134
  93.8 20.8 %all-gather.8.cloned.1.call-done = bf16[2048,768]{1,0:T(8,128)(2,1)} async-done(((bf16[1024,768]{1,0:T(8,128)(2,1)}), bf16[2048,768]{1,0:T(8,128)(2,1)}) %all-gather.8.cloned.1.call-update) | async-done | bytes 3145744 | tf_op jit(solution)/shard_map/all_gather | solution.py:145
  114.7 6.5 convolution_bitcast_fusion
  128.6 5.8 copy.68
  134.4 5.7 copy.70
  140.1 5.2 fusion.129
  148.9 116.7 %while.28 = (s32[]{:T(128)}, bf16[6,2048,64]{1,2,0:T(8,128)(2,1)}, f32[6,2048]{1,0:T(8,128)}, bf16[6,2048,64]{2,1,0:T(8,128)(2,1)}, bf16[6,2048,64]{2,1,0:T(8,12...) while((s32[]{:T(128)}, bf16[6,2048,64]{1,2,0:T(8,128)(2,1)}, ...), condition=%wide.region_10.12_spmd.clone, body=%wide.region_1.11_spmd.clone.sunk | while | flops 1125128192 | bytes 70637272 | solution.py:152
  154.7 3.5 fusion.240
  174.1 3.5 fusion.240
  193.5 3.5 fusion.240
  212.9 3.5 fusion.240
  232.3 3.5 fusion.240
  265.6 6.2 convolution_convert_fusion
  273.5 41.9 %reduce-scatter.9.cloned.1.call-done = bf16[1024,768]{1,0:T(8,128)(2,1)} async-done(((bf16[2048,768]{1,0:T(8,128)(2,1)}), bf16[1024,768]{1,0:T(8,128)(2,1)}) %reduce-scatter.9.cloned.1.call-update) | async-done | bytes 1572880 | tf_op jit(solution)/shard_map/reduce_scatter | solution.py:159
  321.4 39.1 %all-gather.14.cloned.1.call-done = bf16[768,1536]{1,0:T(8,128)(2,1)} async-done(((bf16[48,1536]{1,0:T(8,128)(2,1)}), bf16[768,1536]{1,0:T(8,128)(2,1)}) %all-gather.14.cloned.1.call-update) | async-done | bytes 2359312 | tf_op jit(solution)/shard_map/all_gather | solution.py:135
  360.5 45.1 %all-gather.12.cloned.1.call-done = bf16[2048,768]{1,0:T(8,128)(2,1)} async-done(((bf16[1024,768]{1,0:T(8,128)(2,1)}), bf16[2048,768]{1,0:T(8,128)(2,1)}) %all-gather.12.cloned.1.call-update) | async-done | bytes 3145744 | tf_op jit(solution)/shard_map/all_gather | solution.py:170
  405.5 34.6 %fusion.115 = (bf16[2048,1536]{1,0:T(8,128)(2,1)}, f32[2048,1536]{1,0:T(8,128)}) fusion(f32[1536]{0:T(1024)S(1)} %copy-done.49, bf16[2048,768]{1,0:T(8,128)(2,1)} %all-gather.12.cloned.1.call-done, bf16[768,1536]{1,0:T(8,128)(2,1)} %all-gather.14.cloned.1.call-done), kind=kOutput, calls=%fused_computation.175 | convolution fusion | flops 5039456256 | bytes 24385536 | tf_op jit(solution)/shard_map/dot_general | solution.py:171
  440.1 10.5 all-gather.16.cloned.1.call-done
  450.6 9.0 convolution_convert_fusion.2
  459.7 40.0 %all_to_all.43 = bf16[16,1,64,768]{3,2,1,0:T(8,128)(2,1)S(1)} all-to-all(bf16[16,1,64,768]{3,2,1,0:T(8,128)(2,1)} %get-tuple-element.271), channel_id=1, replica_groups=mesh['dp'=16,'tensor'=2] {'dp'}, dimensions={0} | all-to-all | bytes 3145728 | tf_op jit(solution)/shard_map/all_to_all | solution.py:115
  511.8 45.3 %all-gather.18.cloned.1.call-done = bf16[2048,768]{1,0:T(8,128)(2,1)} async-done(((bf16[1024,768]{1,0:T(8,128)(2,1)}), bf16[2048,768]{1,0:T(8,128)(2,1)}) %all-gather.18.cloned.1.call-update) | async-done | bytes 3145744 | tf_op jit(solution)/shard_map/all_gather | solution.py:194
  557.1 12.4 convert_reduce_fusion
  572.2 6.4 convolution_convert_fusion.1
  578.7 43.5 %reduce-scatter.13.cloned.1.call-done = bf16[1024,768]{1,0:T(8,128)(2,1)} async-done(((bf16[2048,768]{1,0:T(8,128)(2,1)}), bf16[1024,768]{1,0:T(8,128)(2,1)}) %reduce-scatter.13.cloned.1.call-update) | async-done | bytes 1572880 | tf_op jit(solution)/shard_map/reduce_scatter | solution.py:201
  622.2 4.6 multiply_reduce_fusion.4
  632.3 45.0 %all-gather.20.cloned.1.call-done = bf16[2048,768]{1,0:T(8,128)(2,1)} async-done(((bf16[1024,768]{1,0:T(8,128)(2,1)}), bf16[2048,768]{1,0:T(8,128)(2,1)}) %all-gather.20.cloned.1.call-update) | async-done | bytes 3145744 | tf_op jit(solution)/shard_map/all_gather | solution.py:213
  687.4 217.3 %while.29 = (s32[]{:T(128)}, bf16[6,2048,64]{1,2,0:T(8,128)(2,1)}, bf16[6,2048,64]{1,2,0:T(8,128)(2,1)}, bf16[6,2048,64]{1,2,0:T(8,128)(2,1)}, bf16[6,2048,64]{2...) while((s32[]{:T(128)}, bf16[6,2048,64]{1,2,0:T(8,128)(2,1)}, ...), condition=%wide.region_27.29_spmd.clone, body=%wide.region_22.28_spmd.clone.sunk | while | flops 2724331520 | bytes 161284432 | solution.py:218
  910.7 8.5 bitcast_convert_fusion
  921.2 9.6 fusion.157
  932.6 9.5 fusion.156
  943.5 4.8 fusion.155
  948.3 3.8 copy.87
  952.6 11.5 reduce.24
  964.1 4.7 reshape.275
  968.8 5.7 all-to-all-start.1
  974.6 8.7 fusion.138
  989.6 11.5 reduce.23
  1001.1 4.6 reshape.277
  1005.7 9.2 all-to-all-done.1
  1014.9 19.2 %all-to-all-start.3 = ((bf16[16,2,24576]{2,1,0:T(2,128)(2,1)}), bf16[16,2,24576]{2,1,0:T(2,128)(2,1)}, u32[]{:S(2)}, u32[]{:S(2)}) async-start(bf16[16,2,24576]{2,1,0:T(2,128)(2,1)} %reshape.277), calls=%async_computation.7 | async-start | bytes 3145728 | tf_op jit(solution)/shard_map/all_to_all | solution.py:277
  1034.2 10.1 reshape.276
  1052.1 48.7 %all-reduce = (f32[2,768]{1,0:T(2,128)S(1)}, f32[6,768]{1,0:T(8,128)S(1)}, f32[3072]{0:T(1024)S(1)}) all-reduce(f32[2,768]{1,0:T(2,128)S(1)} %maximum_dynamic-update-slice_fusion, f32[6,768]{1,0:T(8,128)S(1)} %stack.44, f32[3072]{0:T(1024)S(1)} %dynamic_update_slice.24), channel_id=1, replica_groups=mesh['dp'=16,'tensor'=2] {'dp','tensor'}, use_global_device_ids=true, to_apply=%region_35.37 | all-reduce | flops 9216 | bytes 73728 | tf_op jit(solution)/shard_map/psum | solution.py:270
  1102.7 8.1 reshape.278
  1115.5 3.5 fusion.145
  1119.0 28.0 %reduce-scatter.21.cloned.1.call-done = f32[48,1536]{1,0:T(8,128)} async-done(((f32[768,1536]{1,0:T(8,128)}), f32[48,1536]{1,0:T(8,128)}) %reduce-scatter.21.cloned.1.call-update) | async-done | bytes 294928 | tf_op jit(solution)/shard_map/reduce_scatter | solution.py:255
  1147.0 61.5 %reduce-scatter.19.cloned.1.call-done = f32[48,384]{1,0:T(8,128)} async-done(((f32[768,384]{1,0:T(8,128)}), f32[48,384]{1,0:T(8,128)}) %reduce-scatter.19.cloned.1.call-update) | async-done | bytes 73744 | tf_op jit(solution)/shard_map/reduce_scatter | solution.py:254
  1208.6 71.4 %reduce-scatter.17.cloned.1.call-done = f32[48,3,384]{2,0,1:T(8,128)} async-done(((f32[768,3,384]{2,0,1:T(8,128)}), f32[48,3,384]{2,0,1:T(8,128)}) %reduce-scatter.17.cloned.1.call-update) | async-done | bytes 221200 | tf_op jit(solution)/shard_map/reduce_scatter | solution.py:253
  (500 shorter events, 405.6 us)
Async XLA Ops:
  7.2 5.0 copy-start
  7.2 86.6 %all-gather.10.cloned.1.call-start = ((), (), s32[]{:S(2)}) async-start(), calls=%async_computation.13 | async-start | bytes 1880064 | tf_op jit(solution)/shard_map/all_gather | solution.py:133
  9.0 105.7 %all-gather.8.cloned.1.call-start = ((), (), s32[]{:S(2)}) async-start(), calls=%async_computation.12 | async-start | bytes 4718592 | tf_op jit(solution)/shard_map/all_gather | solution.py:145
  16.4 53.1 %copy-start.43 = (f32[2,384]{1,0:T(2,128)S(1)}, f32[2,384]{1,0:T(2,128)}, u32[]{:S(2)}) copy-start(f32[2,384]{1,0:T(2,128)} %param.30) | copy-start | bytes 9220
  16.4 53.3 %copy-start.30 = (f32[48,384]{1,0:T(8,128)S(1)}, f32[48,384]{1,0:T(8,128)}, u32[]{:S(2)}) copy-start(f32[48,384]{1,0:T(8,128)} %param.27) | copy-start | bytes 221188
  16.4 53.3 %copy-start.50 = (s32[16]{0:T(128)S(1)}, s32[16]{0:T(128)}, u32[]{:S(2)}) copy-start(s32[16]{0:T(128)} %param.24) | copy-start | bytes 196
  69.4 246.0 %reduce-scatter.9.cloned.1.call-start = ((), (), s32[]{:S(2)}) async-start(), calls=%async_computation.14 | async-start | bytes 4718592 | tf_op jit(solution)/shard_map/reduce_scatter | solution.py:159
  140.1 5.2 copy-start.11
  265.6 6.2 copy-start.2
  271.8 43.6 %copy-start.29 = (f32[768]{0:T(1024)S(1)}, f32[768]{0:T(1024)}, u32[]{:S(2)}) copy-start(f32[768]{0:T(1024)} %param.31) | copy-start | bytes 9220
  271.8 43.6 %copy-start.4 = (bf16[16,1,64,768]{3,2,1,0:T(8,128)(2,1)S(1)}, bf16[16,1,64,768]{3,2,1,0:T(8,128)(2,1)}, u32[]{:S(2)}) copy-start(bf16[16,1,64,768]{3,2,1,0:T(8,128)(2,1)} %all_to_all.42) | copy-start | bytes 4718596
  271.8 88.7 %all-gather.14.cloned.1.call-start = ((), (), s32[]{:S(2)}) async-start(), calls=%async_computation.16 | async-start | bytes 2506752 | tf_op jit(solution)/shard_map/all_gather | solution.py:135
  273.4 45.0 %copy-start.31 = (f32[768]{0:T(1024)S(1)}, f32[768]{0:T(1024)}, u32[]{:S(2)}) copy-start(f32[768]{0:T(1024)} %param.34) | copy-start | bytes 9220
  273.5 45.0 %copy-start.38 = (f32[768]{0:T(1024)S(1)}, f32[768]{0:T(1024)}, u32[]{:S(2)}) copy-start(f32[768]{0:T(1024)} %param.35) | copy-start | bytes 9220
  273.5 132.1 %all-gather.12.cloned.1.call-start = ((), (), s32[]{:S(2)}) async-start(), calls=%async_computation.15 | async-start | bytes 4718592 | tf_op jit(solution)/shard_map/all_gather | solution.py:170
  318.4 87.1 %copy-start.49 = (f32[1536]{0:T(1024)S(1)}, f32[1536]{0:T(1024)}, u32[]{:S(2)}) copy-start(f32[1536]{0:T(1024)} %param.32) | copy-start | bytes 18436
  320.5 130.0 %all-gather.16.cloned.1.call-start = ((), (), s32[]{:S(2)}) async-start(), calls=%async_computation.17 | async-start | bytes 2506752 | tf_op jit(solution)/shard_map/all_gather | solution.py:136
  321.3 181.0 %reduce-scatter.11.cloned.1.call-start = ((), (), s32[]{:S(2)}) async-start(), calls=%async_computation.18 | async-start | bytes 4718592 | tf_op jit(solution)/shard_map/reduce_scatter | solution.py:173
  459.6 41.3 %copy-start.32 = (f32[768]{0:T(1024)S(1)}, f32[768]{0:T(1024)}, u32[]{:S(2)}) copy-start(f32[768]{0:T(1024)} %param.36) | copy-start | bytes 9220
  459.7 42.7 %copy-start.41 = (f32[768]{0:T(1024)S(1)}, f32[768]{0:T(1024)}, u32[]{:S(2)}) copy-start(f32[768]{0:T(1024)} %param.33) | copy-start | bytes 9220
  459.7 97.4 %all-gather.18.cloned.1.call-start = ((), (), s32[]{:S(2)}) async-start(), calls=%async_computation.19 | async-start | bytes 4718592 | tf_op jit(solution)/shard_map/all_gather | solution.py:194
  511.8 110.4 %reduce-scatter.13.cloned.1.call-start = ((), (), s32[]{:S(2)}) async-start(), calls=%async_computation.20 | async-start | bytes 4718592 | tf_op jit(solution)/shard_map/reduce_scatter | solution.py:201
  557.1 15.1 %copy-start.48 = (bf16[768,1536]{1,0:T(8,128)(2,1)S(1)}, bf16[768,1536]{1,0:T(8,128)(2,1)}, u32[]{:S(2)}) copy-start(bf16[768,1536]{1,0:T(8,128)(2,1)} %all-gather.14.cloned.1.call-done) | copy-start | bytes 7077892
  578.6 98.7 %all-gather.20.cloned.1.call-start = ((), (), s32[]{:S(2)}) async-start(), calls=%async_computation.21 | async-start | bytes 4718592 | tf_op jit(solution)/shard_map/all_gather | solution.py:213
  622.2 4.6 copy-start.10
  622.2 4.6 copy-start.21
  630.9 46.4 %copy-start.26 = (bf16[768,384]{1,0:T(8,128)(2,1)S(1)}, bf16[768,384]{1,0:T(8,128)(2,1)}, u32[]{:S(2)}) copy-start(bf16[768,384]{1,0:T(8,128)(2,1)} %all_gather.30) | copy-start | bytes 1769476
  632.2 351.1 %reduce-scatter.15.cloned.1.call-start = ((), (), s32[]{:S(2)}) async-start(), calls=%async_computation.22 | async-start | bytes 4718592 | tf_op jit(solution)/shard_map/reduce_scatter | solution.py:244
  904.7 4.4 copy-start.14
  919.3 199.7 %reduce-scatter.23.cloned.1.call-start = ((), (), s32[]{:S(2)}) async-start(), calls=%async_computation.26 | async-start | bytes 5013504 | tf_op jit(solution)/shard_map/reduce_scatter | solution.py:256
  930.8 216.3 %reduce-scatter.21.cloned.1.call-start = ((), (), s32[]{:S(2)}) async-start(), calls=%async_computation.25 | async-start | bytes 5013504 | tf_op jit(solution)/shard_map/reduce_scatter | solution.py:255
  942.1 266.5 %reduce-scatter.19.cloned.1.call-start = ((), (), s32[]{:S(2)}) async-start(), calls=%async_computation.24 | async-start | bytes 1253376 | tf_op jit(solution)/shard_map/reduce_scatter | solution.py:254
  964.1 10.4 copy-start.23
  964.1 10.4 copy-start.24
  968.8 46.1 %all-to-all-start.1 = ((bf16[16,2,24576]{2,1,0:T(2,128)(2,1)}), bf16[16,2,24576]{2,1,0:T(2,128)(2,1)}, u32[]{:S(2)}, u32[]{:S(2)}) async-start(bf16[16,2,24576]{2,1,0:T(2,128)(2,1)} %reshape.275), calls=%async_computation.3 | async-start | bytes 3145728 | tf_op jit(solution)/shard_map/all_to_all | solution.py:274
  974.5 305.5 %reduce-scatter.17.cloned.1.call-start = ((), (), s32[]{:S(2)}) async-start(), calls=%async_computation.23 | async-start | bytes 3760128 | tf_op jit(solution)/shard_map/reduce_scatter | solution.py:253
  1001.1 33.0 %copy-start.45 = (s32[16]{0:T(128)S(1)}, s32[16]{0:T(128)}, u32[]{:S(2)}) copy-start(s32[16]{0:T(128)} %get-tuple-element.277) | copy-start | bytes 196
  1001.1 33.1 %copy-start.36 = (f32[768]{0:T(1024)S(1)}, f32[768]{0:T(1024)}, u32[]{:S(2)}) copy-start(f32[768]{0:T(1024)} %get-tuple-element.194) | copy-start | bytes 9220
  1001.1 33.1 %copy-start.39 = (f32[768]{0:T(1024)S(1)}, f32[768]{0:T(1024)}, u32[]{:S(2)}) copy-start(f32[768]{0:T(1024)} %get-tuple-element.189) | copy-start | bytes 9220
  1014.9 87.7 %all-to-all-start.3 = ((bf16[16,2,24576]{2,1,0:T(2,128)(2,1)}), bf16[16,2,24576]{2,1,0:T(2,128)(2,1)}, u32[]{:S(2)}, u32[]{:S(2)}) async-start(bf16[16,2,24576]{2,1,0:T(2,128)(2,1)} %reshape.277), calls=%async_computation.7 | async-start | bytes 3145728 | tf_op jit(solution)/shard_map/all_to_all | solution.py:277
  1044.3 6.8 copy-start.40
  1044.3 7.1 copy-start.35
  1044.3 7.1 copy-start.34
  1044.3 7.1 copy-start.33
  1044.3 7.1 copy-start.37
  1044.3 7.2 copy-start.17
  1110.8 4.7 copy-start.44
  1115.5 164.5 %copy-start.1 = (bf16[16,1,64,768]{3,2,1,0:T(8,128)(2,1)S(1)}, bf16[16,1,64,768]{3,2,1,0:T(8,128)(2,1)}, u32[]{:S(2)}) copy-start(bf16[16,1,64,768]{3,2,1,0:T(8,128)(2,1)} %param.23) | copy-start | bytes 4718596
  (41 other events, 102.0 us)
Sparse Core Ops, SparseCore 0:
  10.9 53.5 all-gather.9
  69.5 45.1 all-gather.7
  271.9 43.4 reduce-scatter.8
  318.1 42.3 all-gather.13
  361.9 43.6 all-gather.11
  408.2 42.3 all-gather.15
  459.8 42.1 reduce-scatter.10
  511.9 45.1 all-gather.17
  578.7 43.4 reduce-scatter.12
  632.3 44.8 all-gather.19
  919.4 43.3 reduce-scatter.14
  967.1 94.6 reduce-scatter.22
  1066.2 80.7 reduce-scatter.20
  1151.1 57.4 reduce-scatter.18
  1212.9 67.0 reduce-scatter.16
where the time goes:
time: 1300 us; the launch traced here: 1290 us
  waiting for transfers between devices  462 us (36%)
  matrix products  388 us (30%)
  blocking collectives  165 us (13%)
  local copies, waits for them, and re-layouts  116 us (9%)
  other arithmetic  113 us (9%)
  starting transfers between devices  25.9 us (2%)
  between operations  14.7 us (1%)
    dot_general x75, matrix products, contract_last(): lax.dot_general(left_side, right_side, (((1,), (1,)), ((), ())), preferre...  168 us
    dot_general x51, matrix products, contract_first(): lax.dot_general(left_side, right_side, (((0,), (0,)), ((), ())), preferre...  97.7 us
    reduce_scatter x1, waiting for transfers between devices, per_device(): lax.psum_scatter(qkv_weight_grad, 'dp', scatter_dimension=0, tiled=True)  71.4 us
    reduce_scatter x1, waiting for transfers between devices, per_device(): lax.psum_scatter(out_weight_grad, 'dp', scatter_dimension=0, tiled=True)  61.5 us
    all_to_all x1, blocking collectives, per_device(): lax.all_to_all(jnp.take(x_in, owners, axis=0), 'dp', split_axis=0, concat...  53 us
    psum x1, blocking collectives, per_device(): lax.psum((norm_terms, qv_padded, in_padded), ('dp', 'tensor'))  48.7 us
    unnamed x103, local copies, waits for them, and re-layouts  46.6 us
    all_gather x1, waiting for transfers between devices, per_device(): lax.all_gather(final_grad.astype(jnp.bfloat16), 'tensor', axis=0, tiled=T...  45.3 us
  transfers between devices with their start and end apart: 17, of which 12 were waited for; matrix products, arithmetic and copies ran while one was open for 12% of the time, Pallas kernels for 0%

commit v1 on v0

v1 whole, which is shorter than its diff:
```python
import functools

import jax
import jax.numpy as jnp
from jax import lax
from jax.experimental import pallas as pl
from jax.experimental.pallas import tpu as pltpu
from jax.sharding import PartitionSpec as P

LOG2E = 1.4426950408889634
MASKED = -1e30
HEAD_DIM = 64
PAIR = 2 * HEAD_DIM


def contract_last(a, b):
    return lax.dot_general(a, b, (((1,), (1,)), ((), ())), preferred_element_type=jnp.float32)


def lane_iota(shape):
    return lax.broadcasted_iota(jnp.int32, shape, len(shape) - 1)


def attn_fwd_kernel(scale, len_ref, q_ref, k_ref, v_ref, o_ref, lse_ref, kx, vx):
    keys = k_ref.shape[0]
    rows = q_ref.shape[0]

    @pl.when(pl.program_id(1) == 0)
    def _():
        lanes = lane_iota((keys, PAIR))
        valid = lax.broadcasted_iota(jnp.int32, (keys, PAIR), 0) < len_ref[0]
        bias = jnp.where(valid, 0.0, MASKED)
        k2 = k_ref[...].astype(jnp.float32)
        v2 = v_ref[...].astype(jnp.float32)
        for h in range(2):
            mine = (lanes // HEAD_DIM) == h
            spare = lanes == (1 - h) * HEAD_DIM
            kx[h] = jnp.where(mine, k2, jnp.where(spare, bias, 0.0)).astype(jnp.bfloat16)
            vx[h] = jnp.where(mine, v2, 1.0).astype(jnp.bfloat16)

    lanes = lane_iota((rows, PAIR))
    q2 = q_ref[...].astype(jnp.float32)
    low = lanes < HEAD_DIM
    sums, tops = [], []
    for h in range(2):
        mine = (lanes // HEAD_DIM) == h
        spare = lanes == (1 - h) * HEAD_DIM
        qx = jnp.where(mine, q2, jnp.where(spare, 1.0, 0.0)).astype(jnp.bfloat16)
        s = contract_last(qx, kx[h])
        top = jnp.max(s, axis=1, keepdims=True)
        p = jnp.exp2(s * scale - top * scale).astype(jnp.bfloat16)
        sums.append(jnp.dot(p, vx[h], preferred_element_type=jnp.float32))
        tops.append(top * scale)
    num = jnp.where(low, sums[0], sums[1])
    den = pltpu.roll(jnp.where(low, sums[1], sums[0]), HEAD_DIM, 1)
    o_ref[...] = (num / den).astype(jnp.bfloat16)
    lse_ref[...] = jnp.where(low, tops[0], tops[1]) + jnp.log2(den)


def attn_fwd(length, q, kv, block):
    rows, width = q.shape
    keys = kv.shape[0]
    pairs = width // PAIR
    return pl.pallas_call(
        functools.partial(attn_fwd_kernel, LOG2E * HEAD_DIM ** -0.5),
        grid_spec=pltpu.PrefetchScalarGridSpec(
            num_scalar_prefetch=1,
            grid=(pairs, rows // block),
            in_specs=[
                pl.BlockSpec((block, PAIR), lambda p, i, n: (i, p)),
                pl.BlockSpec((keys, PAIR), lambda p, i, n: (0, p)),
                pl.BlockSpec((keys, PAIR), lambda p, i, n: (0, pairs + p)),
            ],
            out_specs=[
                pl.BlockSpec((block, PAIR), lambda p, i, n: (i, p)),
                pl.BlockSpec((block, PAIR), lambda p, i, n: (i, p)),
            ],
            scratch_shapes=[
                pltpu.VMEM((2, keys, PAIR), jnp.bfloat16),
                pltpu.VMEM((2, keys, PAIR), jnp.bfloat16),
            ],
        ),
        out_shape=[
            jax.ShapeDtypeStruct((rows, width), jnp.bfloat16),
            jax.ShapeDtypeStruct((rows, width), jnp.float32),
        ],
        name="attn_fwd",
        cost_estimate=pl.CostEstimate(flops=4 * rows * keys * width * 4, bytes_accessed=10_000_000, transcendentals=rows * keys * width // 64),
    )(length, q, kv, kv)


def split3(x):
    a = x.astype(jnp.bfloat16).astype(jnp.float32)
    b = (x - a).astype(jnp.bfloat16).astype(jnp.float32)
    return a, b, x - a - b


def attn_bwd_kernel(scale, len_ref, q_ref, k_ref, v_ref, o_ref, lse_ref, g_ref, dq_ref, dk_ref, dv_ref, qx, gx, qz, gz, dqt):
    rows = q_ref.shape[0]
    keys = k_ref.shape[0]
    c = pl.program_id(1)

    @pl.when(c == 0)
    def _():
        lanes = lane_iota((rows, PAIR))
        q2 = q_ref[...].astype(jnp.float32)
        g2 = g_ref[...].astype(jnp.float32)
        go = g2 * o_ref[...].astype(jnp.float32)
        other = -pltpu.roll(lse_ref[...], HEAD_DIM, 1) * (1.0 / scale)
        a, b, d = split3(other)
        for h in range(2):
            mine = (lanes // HEAD_DIM) == h
            base = (1 - h) * HEAD_DIM
            delta = -jnp.sum(jnp.where(mine, go, 0.0), axis=1, keepdims=True)
            da, db, dd = split3(delta)
            ext = jnp.where(lanes == base, a, jnp.where(lanes == base + 1, b, jnp.where(lanes == base + 2, d, jnp.where(lanes == base + 3, 1.0, 0.0))))
            qx[h] = jnp.where(mine, q2, ext).astype(jnp.bfloat16)
            qz[h] = jnp.where(mine, q2, 0.0).astype(jnp.bfloat16)
            ext = jnp.where(lanes == base, da, jnp.where(lanes == base + 1, db, jnp.where(lanes == base + 2, dd, 0.0)))
            gx[h] = jnp.where(mine, g2, ext).astype(jnp.bfloat16)
            gz[h] = jnp.where(mine, g2, 0.0).astype(jnp.bfloat16)
        dqt[...] = jnp.zeros_like(dqt)

    lanes = lane_iota((keys, PAIR))
    valid = lax.broadcasted_iota(jnp.int32, (keys, PAIR), 0) + c * keys < len_ref[0]
    bias = jnp.where(valid, 0.0, MASKED)
    k2 = k_ref[...].astype(jnp.float32)
    v2 = v_ref[...].astype(jnp.float32)
    kt = k2.T.astype(jnp.bfloat16)
    dv = None
    dk = None
    for h in range(2):
        mine = (lanes // HEAD_DIM) == h
        base = (1 - h) * HEAD_DIM
        ones = jnp.where((lanes >= base) & (lanes < base + 3), 1.0, 0.0)
        kx = jnp.where(mine, k2, jnp.where(lanes == base + 3, bias, ones)).astype(jnp.bfloat16)
        vx = jnp.where(mine, v2, ones).astype(jnp.bfloat16)
        s = contract_last(kx, qx[h])
        p = jnp.exp2(s * scale)
        da = contract_last(vx, gx[h])
        ds = (p * da).astype(jnp.bfloat16)
        dv_h = jnp.dot(p.astype(jnp.bfloat16), gz[h], preferred_element_type=jnp.float32)
        dk_h = jnp.dot(ds, qz[h], preferred_element_type=jnp.float32)
        dv = dv_h if dv is None else dv + dv_h
        dk = dk_h if dk is None else dk + dk_h
        half = pl.ds(h * HEAD_DIM, HEAD_DIM)
        dqt[half, :] += jnp.dot(kt[h * HEAD_DIM : (h + 1) * HEAD_DIM], ds, preferred_element_type=jnp.float32)
    root = HEAD_DIM ** -0.5
    dk_ref[...] = (dk * root).astype(jnp.bfloat16)
    dv_ref[...] = dv.astype(jnp.bfloat16)

    @pl.when(c == pl.num_programs(1) - 1)
    def _():
        dq_ref[...] = (dqt[...] * root).T.astype(jnp.bfloat16)


def attn_bwd(length, q, kv, o, lse, g, block):
    rows, width = q.shape
    keys = kv.shape[0]
    pairs = width // PAIR
    whole = pl.BlockSpec((rows, PAIR), lambda p, i, n: (0, p))
    part = pl.BlockSpec((block, PAIR), lambda p, i, n: (i, p))
    late = pl.BlockSpec((block, PAIR), lambda p, i, n: (i, pairs + p))
    out = pl.pallas_call(
        functools.partial(attn_bwd_kernel, LOG2E * HEAD_DIM ** -0.5),
        grid_spec=pltpu.PrefetchScalarGridSpec(
            num_scalar_prefetch=1,
            grid=(pairs, keys // block),
            in_specs=[whole, part, late, whole, whole, whole],
            out_specs=[whole, part, part],
            scratch_shapes=[pltpu.VMEM((2, rows, PAIR), jnp.bfloat16)] * 4
            + [pltpu.VMEM((PAIR, rows), jnp.float32)],
        ),
        out_shape=[
            jax.ShapeDtypeStruct((rows, width), jnp.bfloat16),
            jax.ShapeDtypeStruct((keys, width), jnp.bfloat16),
            jax.ShapeDtypeStruct((keys, width), jnp.bfloat16),
        ],
        name="attn_bwd",
        cost_estimate=pl.CostEstimate(flops=10 * rows * keys * width * 4, bytes_accessed=20_000_000, transcendentals=rows * keys * width // 64),
    )(length, q, kv, kv, o, lse, g)
    return out


def contract_first(a, b):
    return lax.dot_general(a, b, (((0,), (0,)), ((), ())), preferred_element_type=jnp.float32)


def dense(a, b):
    return jnp.dot(a, b, preferred_element_type=jnp.float32)


def norm_forward(values, norm_gain, norm_shift):
    centre = jnp.mean(values, axis=-1, keepdims=True)
    centred = values - centre
    inverse = lax.rsqrt(jnp.mean(centred * centred, axis=-1, keepdims=True) + 1e-06)
    normed = centred * inverse
    return (normed * norm_gain + norm_shift, normed, inverse)


def norm_backward(upstream, normed, inverse, norm_gain):
    scaled = upstream * norm_gain
    back_rows = inverse * (
        scaled
        - jnp.mean(scaled, axis=-1, keepdims=True)
        - normed * jnp.mean(scaled * normed, axis=-1, keepdims=True)
    )
    return (back_rows, jnp.sum(upstream * normed, axis=0), jnp.sum(upstream, axis=0))


def gelu_slope(values):
    return (
        0.5 * (1.0 + lax.erf(values * 0.7071067811865476))
        + values * jnp.exp(-0.5 * values * values) * 0.3989422804014327
    )


def deal(blocks):
    out = lax.all_to_all(blocks, "dp", split_axis=0, concat_axis=0, tiled=True)
    return out.reshape(-1, out.shape[-1])


def undeal(rows):
    blocks = rows.reshape(lax.axis_size("dp"), -1, rows.shape[-1])
    return lax.all_to_all(blocks, "dp", split_axis=0, concat_axis=0, tiled=True)[:, None]


def gather_weight(weight):
    low = lax.all_gather(weight.astype(jnp.bfloat16), "tensor", axis=weight.ndim - 1, tiled=True)
    return lax.all_gather(low, "dp", axis=0, tiled=True)


def scatter_weight(grad):
    part = lax.psum_scatter(grad.astype(jnp.bfloat16), "dp", scatter_dimension=0, tiled=True)
    return lax.psum_scatter(
        part.astype(jnp.float32), "tensor", scatter_dimension=grad.ndim - 1, tiled=True
    )


def per_device(
    x_in, cotangent, lengths, dealing, w_qkv, w_out, w_in, w_ffo,
    b_qv, b_out, b_in, b_ffo, ln1_gain, ln1_bias, ln2_gain, ln2_bias,
):
    low = jnp.bfloat16
    tensor_index = lax.axis_index("tensor")
    width = x_in.shape[-1]
    length = lengths[dealing[lax.axis_index("dp")]][None].astype(jnp.int32)
    qkv_weight = gather_weight(w_qkv)
    biases = lax.all_gather(
        jnp.concatenate([b_qv.reshape(-1), b_in]), "tensor", axis=0, tiled=False
    )
    split = 2 * b_qv.shape[1]
    qv_bias = biases[:, :split].reshape(-1, 2, b_qv.shape[1]).transpose(1, 0, 2).reshape(2, -1)
    in_bias = biases[:, split:].reshape(-1)
    tokens_half = deal(x_in[:, 0])
    half_rows = tokens_half.shape[0]
    tokens_full = lax.all_gather(tokens_half, "tensor", axis=0, tiled=True)
    out_weight = gather_weight(w_out)
    in_weight = gather_weight(w_in)
    ffo_weight = gather_weight(w_ffo)
    q_weight = qkv_weight[:, 0]
    kv_weight = qkv_weight[:, 1:].reshape(width, -1)
    query = (dense(tokens_half, q_weight) + qv_bias[0]).astype(low)
    kv_bias = jnp.concatenate([jnp.zeros((width,), jnp.float32), qv_bias[1]])
    keyval = (dense(tokens_full, kv_weight) + kv_bias).astype(low)
    mixed, totals = attn_fwd(length, query, keyval, 256)
    attn_half = contract_last(mixed, out_weight)
    first_norm, normed_one, inverse_one = norm_forward(
        tokens_half.astype(jnp.float32) + attn_half + b_out, ln1_gain, ln1_bias
    )
    first_low = first_norm.astype(low)
    hidden = dense(first_low, in_weight) + in_bias
    active = jax.nn.gelu(hidden, approximate=False).astype(low)
    result, normed_two, inverse_two = norm_forward(
        first_norm + contract_last(active, ffo_weight) + b_ffo, ln2_gain, ln2_bias
    )
    output_grad = deal(cotangent[:, 0]).astype(jnp.float32)
    final_grad, gain_two_grad, shift_two_grad = norm_backward(
        output_grad, normed_two, inverse_two, ln2_gain
    )
    ffo_bias_grad = jnp.sum(final_grad, axis=0)
    final_low = final_grad.astype(low)
    ffo_sum = scatter_weight(contract_first(final_low, active))
    hidden_grad = (dense(final_low, ffo_weight) * gelu_slope(hidden)).astype(low)
    in_sum = scatter_weight(contract_first(first_low, hidden_grad))
    in_bias_grad = jnp.sum(hidden_grad.astype(jnp.float32), axis=0)
    first_grad = final_grad + contract_last(hidden_grad, in_weight)
    resid_grad, gain_one_grad, shift_one_grad = norm_backward(
        first_grad, normed_one, inverse_one, ln1_gain
    )
    out_bias_grad = jnp.sum(resid_grad, axis=0)
    resid_low = resid_grad.astype(low)
    out_sum = scatter_weight(contract_first(resid_low, mixed))
    mixed_grad = dense(resid_low, out_weight).astype(low)
    dq, dk, dv = attn_bwd(length, query, keyval, mixed, totals, mixed_grad, 512)
    q_bias_grad = jnp.sum(dq.astype(jnp.float32), axis=0)
    v_bias_grad = jnp.sum(dv.astype(jnp.float32), axis=0)
    qkv_grad = jnp.stack(
        [
            contract_first(tokens_half, dq),
            contract_first(tokens_full, dk),
            contract_first(tokens_full, dv),
        ],
        axis=1,
    )
    qkv_sum = scatter_weight(qkv_grad)
    shared = contract_last(dk, qkv_weight[:, 1]) + contract_last(dv, qkv_weight[:, 2])
    own = lax.psum_scatter(shared.astype(low), "tensor", scatter_dimension=0, tiled=True)
    input_grad = resid_grad + contract_last(dq, q_weight) + own.astype(jnp.float32)
    terms = jnp.concatenate(
        [
            out_bias_grad, ffo_bias_grad, gain_one_grad, shift_one_grad,
            gain_two_grad, shift_two_grad, q_bias_grad, v_bias_grad, in_bias_grad,
        ]
    )
    sums = lax.psum(terms, ("dp", "tensor"))
    norm_sums = sums[: 6 * width].reshape(6, width)
    qv_sums = sums[6 * width : 8 * width].reshape(2, width)
    share = b_qv.shape[1]
    qv_share = lax.dynamic_slice_in_dim(qv_sums, tensor_index * share, share, 1)
    share = b_in.shape[0]
    in_share = lax.dynamic_slice_in_dim(sums[8 * width :], tensor_index * share, share, 0)
    return (
        undeal(result.astype(low)),
        undeal(input_grad.astype(low)),
        qkv_sum,
        out_sum,
        in_sum,
        ffo_sum,
        qv_share,
        norm_sums[0],
        in_share,
        norm_sums[1],
        norm_sums[2],
        norm_sums[3],
        norm_sums[4],
        norm_sums[5],
    )


def solution(mesh):
    tokens = P(None, "tensor", "dp", None)
    return jax.shard_map(
        per_device,
        mesh=mesh,
        in_specs=(
            tokens, tokens, P(), P(),
            P("dp", None, "tensor"), P("dp", "tensor"), P("dp", "tensor"), P("dp", "tensor"),
            P(None, "tensor"), P(), P("tensor"), P(), P(), P(), P(), P(),
        ),
        out_specs=(
            tokens, tokens,
            P("dp", None, "tensor"), P("dp", "tensor"), P("dp", "tensor"), P("dp", "tensor"),
            P(None, "tensor"), P(), P("tensor"), P(), P(), P(), P(), P(),
        ),
        check_vma=False,
    )
```

time: 1300 us -> 898 us (0.69)
  matrix products: 388 us -> 139 us
  Pallas kernels: 0 us -> 125 us
  other arithmetic: 113 us -> 20.2 us
  waiting for transfers between devices: 462 us -> 373 us
  local copies, waits for them, and re-layouts: 116 us -> 63.3 us
  blocking collectives: 165 us -> 138 us
    dot_general x180 -> x17, matrix products: 388 us -> 139 us  [the longest x5 67.8 us: dense(): return jnp.dot(a, b, preferred_element_type=jnp.float32)]
    all_gather x6 -> x4, waiting for transfers between devices: 185 us -> 36.7 us  [gather_weight(): return lax.all_gather(low, 'dp', axis=0, tiled=True)]
    pallas_call x0 -> x2, Pallas kernels: none -> 125 us  [the longest x1 76.2 us: attn_bwd(): pl.pallas_call(functools.partial(attn_bwd_kernel, LOG2E * HEAD_DIM ** (-0...]
    unnamed x15 -> x16, waiting for transfers between devices: 0.25 us -> 88.7 us
    all_to_all x2 -> x1, blocking collectives: 93 us -> 63.2 us  [deal(): out = lax.all_to_all(blocks, 'dp', split_axis=0, concat_axis=0, tiled=True)]
    unnamed x3 -> x2, other arithmetic: 26.5 us -> 0.01 us
    all_gather x1, waiting for transfers between devices: 20.8 us -> 0.01 us  [per_device(): tokens_full = lax.all_gather(tokens_half, 'tensor', axis=0, tiled=True)]
    reduce_sum x11 -> x3, other arithmetic: 23.7 us -> 7.19 us  [the longest x1 3.1 us: per_device(): ffo_bias_grad = jnp.sum(final_grad, axis=0)]
  transfers between devices with their start and end apart: 17 -> 17, of which waited for: 12 -> 9; matrix products, arithmetic and copies ran while one was open for 12% -> 18% of each run, Pallas kernels for 0% -> 6%
where the time goes in v1:
time: 898 us; the launch traced here: 889 us
  waiting for transfers between devices  373 us (42%)
  matrix products  139 us (15%)
  blocking collectives  138 us (15%)
  Pallas kernels  125 us (14%)
  local copies, waits for them, and re-layouts  63.3 us (7%)
  other arithmetic  20.2 us (2%)
  between operations  17.5 us (2%)
  starting transfers between devices  14.4 us (2%)
    reduce_scatter x3, waiting for transfers between devices, scatter_weight(): lax.psum_scatter(grad.astype(jnp.bfloat16), 'dp', scatter_dimension=0, ti...  209 us
    unnamed x16, waiting for transfers between devices  88.7 us
    pallas_call x1, Pallas kernels, attn_bwd(): pl.pallas_call(functools.partial(attn_bwd_kernel, LOG2E * HEAD_DIM ** (-0...  76.2 us
    dot_general x5, matrix products, dense(): return jnp.dot(a, b, preferred_element_type=jnp.float32)  67.8 us
    all_to_all x1, blocking collectives, deal(): out = lax.all_to_all(blocks, 'dp', split_axis=0, concat_axis=0, tiled=True)  63.2 us
    unnamed x100, local copies, waits for them, and re-layouts  50.4 us
    pallas_call x1, Pallas kernels, attn_fwd(): pl.pallas_call(functools.partial(attn_fwd_kernel, LOG2E * HEAD_DIM ** (-0...  49.2 us
    psum x1, blocking collectives, per_device(): sums = lax.psum(terms, ('dp', 'tensor'))  40.2 us
  transfers between devices with their start and end apart: 17, of which 9 were waited for; matrix products, arithmetic and copies ran while one was open for 18% of the time, Pallas kernels for 6%

profile of v1, /device:TPU:0, one launch (start us, length us, event | category | flops | bytes accessed | tf_op | source)
XLA Modules:
  0.0 889.4 jit_solution(12777314933450807695)
XLA Ops:
  8.2 6.8 all_gather.33
  15.1 63.2 %all_to_all.20 = bf16[16,64,768]{2,1,0:T(8,128)(2,1)} all-to-all(bf16[16,64,768]{2,1,0:T(8,128)(2,1)} %bitcast.87), channel_id=1, replica_groups=mesh['dp'=16,'tensor'=2] {'dp'}, dimensions={0} | all-to-all | bytes 3145728 | tf_op jit(solution)/shard_map/all_to_all | solution.py:219
  78.5 4.8 all_gather.38
  83.4 6.9 all_gather.40
  90.3 4.2 all-to-all-start.2
  94.6 11.0 %all_gather.42 = bf16[48,3072]{1,0:T(8,128)(2,1)} all-gather(bf16[48,1536]{1,0:T(8,128)(2,1)S(1)} %convert_element_type.100), channel_id=1, replica_groups=mesh['dp'=16,'tensor'=2] {'tensor'}, dimensions={1}, use_global_device_ids=true | all-gather | bytes 442368 | tf_op jit(solution)/shard_map/all_gather | solution.py:229
  107.6 4.7 all-gather.1
  113.7 12.7 %all-to-all-done.2 = bf16[16,64,768]{2,1,0:T(8,128)(2,1)S(1)} async-done(((bf16[16,64,768]{2,1,0:T(8,128)(2,1)}), bf16[16,64,768]{2,1,0:T(8,128)(2,1)S(1)}, u32[]{:S(2)}, u32[]{:S(2)}) %all-to-all-start.2) | async-done | bytes 1572896 | tf_op jit(solution)/shard_map/all_to_all | solution.py:219
  128.4 3.3 slice.93
  131.7 4.4 copy.43
  136.1 3.8 add_convert_fusion.4.q_ref
  139.9 9.2 %add_convert_fusion.k_ref.v_ref = bf16[2048,1536]{1,0:T(8,128)(2,1)} fusion(bf16[2048,768]{1,0:T(8,128)(2,1)} %all-gather.10.cloned.1.call-done, bf16[768,1536]{0,1:T(8,128)(2,1)} %bitcast.86, f32[1536]{0:T(1024)S(1)} %concatenate.10), kind=kOutput, calls=%fused_computation.25 | convolution fusion | flops 4838129664 | bytes 11802624 | tf_op jit(solution)/shard_map/dot_general | solution.py:190
  149.1 49.2 %attn_fwd.1 = (bf16[1024,768]{1,0:T(8,128)(2,1)}, f32[1024,768]{1,0:T(8,128)}) custom-call(s32[1]{0:T(128)} %dynamic_slice.13.len_ref, bf16[1024,768]{1,0:T(8,128)(2,1)} %add_convert_fusion.4.q_ref, bf16[2048,1536]{1,0:T(8,128)(2,1)} %add_convert_fusion.k_ref.v_ref, bf16[2048,1536]{1,0:T(8,128)(2,1)} %add_convert_fusion.k_ref.v_ref), custom_call_target="tpu_custom_call" | custom-call | flops 25769803776 | bytes 10000000 | tf_op jit(solution)/shard_map/attn_fwd/pallas_call | solution.py:64
  198.3 3.8 fusion.39
  202.6 20.1 %all-gather.14.cloned.1.call-done = bf16[768,3072]{1,0:T(8,128)(2,1)} async-done(((bf16[48,3072]{1,0:T(8,128)(2,1)}), bf16[768,3072]{1,0:T(8,128)(2,1)}) %all-gather.14.cloned.1.call-update) | async-done | bytes 4718608 | tf_op jit(solution)/shard_map/all_gather | solution.py:230
  222.7 37.2 %fusion.2 = (bf16[1024,3072]{1,0:T(8,128)(2,1)}, f32[1024,3072]{1,0:T(8,128)}) fusion(f32[3072]{0:T(1024)S(1)} %add.147, bf16[768,3072]{1,0:T(8,128)(2,1)} %all-gather.14.cloned.1.call-done, f32[1024,768]{1,0:T(8,128)S(1)} %get-tuple-element.102, f32[768]{0:T(1024)S(1)} %copy-done.33, f32[768]{0:T(1024)S(1)} %copy-done.24, f32[1024]{0:T(1024)S(1)} %add_rsqrt_fusion.1, ...), kind=kOutput, calls=%fused_computation.4 | convolution fusion | flops 5043388416 | bytes 26765312 | tf_op jit(solution)/shard_map/dot_general | solution.py:190
  259.9 16.7 %all-gather.16.cloned.1.call-done = bf16[768,3072]{1,0:T(8,128)(2,1)} async-done(((bf16[48,3072]{1,0:T(8,128)(2,1)}), bf16[768,3072]{1,0:T(8,128)(2,1)}) %all-gather.16.cloned.1.call-update) | async-done | bytes 4718608 | tf_op jit(solution)/shard_map/all_gather | solution.py:230
  276.6 8.9 %fusion.40 = (f32[1024]{0:T(1024)S(1)}, f32[1024,768]{1,0:T(8,128)S(1)}) fusion(f32[768]{0:T(1024)S(1)} %copy-done.32, bf16[1024,3072]{1,0:T(8,128)(2,1)} %get-tuple-element.103, bf16[768,3072]{1,0:T(8,128)(2,1)} %all-gather.16.cloned.1.call-done, f32[768]{0:T(1024)S(1)} %copy-done.33, f32[768]{0:T(1024)S(1)} %copy-done.24, f32[1024]{0:T(1024)S(1)} %add_rsqrt_fusion.1, ...), kind=kOutput, calls=%fused_computation.105 | convolution fusion | flops 4837342208 | bytes 17323008 | tf_op jit(solution)/shard_map/dot_general | solution.py:17
  288.7 3.1 fusion.35
  291.8 15.1 %convert_reduce_fusion = (f32[3072]{0:T(1024)}, bf16[1024,3072]{1,0:T(8,128)(2,1)}) fusion(f32[1024,3072]{1,0:T(8,128)} %get-tuple-element.104, f32[3072]{0:T(1024)S(1)} %add.147, bf16[768,3072]{1,0:T(8,128)(2,1)S(1)} %copy-done.28, f32[1024,768]{1,0:T(8,128)S(1)} %get-tuple-element.91), kind=kOutput, calls=%fused_computation.11 | convolution fusion | flops 4873516032 | bytes 26763264 | tf_op jit(solution)/shard_map/dot_general | solution.py:190
  306.8 8.9 multiply_reduce_fusion
  317.0 2.6 convolution_convert_fusion.2.g_ref
  319.6 76.2 %attn_bwd.1 = (bf16[1024,768]{1,0:T(8,128)(2,1)}, bf16[2048,768]{1,0:T(8,128)(2,1)}, bf16[2048,768]{1,0:T(8,128)(2,1)}) custom-call(s32[1]{0:T(128)} %dynamic_slice.13.len_ref, bf16[1024,768]{1,0:T(8,128)(2,1)} %add_convert_fusion.4.q_ref, bf16[2048,1536]{1,0:T(8,128)(2,1)} %add_convert_fusion.k_ref.v_ref, bf16[2048,1536]{1,0:T(8,128)(2,1)} %add_convert_fusion.k_ref.v_ref, ...), custom_call_target="tpu_custom_call" | custom-call | flops 64424509440 | bytes 20000000 | tf_op jit(solution)/shard_map/attn_bwd/pallas_call | solution.py:164
  395.8 3.0 fusion.24
  399.1 2.8 fusion.26
  401.9 2.8 fusion.25
  405.2 5.7 copy.37
  410.9 5.2 fusion.27
  416.1 5.4 add_convert_fusion.1
  421.8 5.0 convolution_convert_fusion.3
  426.9 10.1 %convolution_convert_fusion.1 = bf16[768,3072]{1,0:T(8,128)(2,1)} fusion(bf16[1024,3072]{1,0:T(8,128)(2,1)} %get-tuple-element.109, f32[1024,768]{1,0:T(8,128)S(1)} %copy-done.3, f32[768]{0:T(1024)S(1)} %copy-done.34, f32[768]{0:T(1024)S(1)} %copy-done.24, f32[1024]{0:T(1024)S(1)} %add_rsqrt_fusion.1, f32[1024]{0:T(1024)S(1)} %broadcast_multiply_fusion.5), kind=kOutput, calls=%fused_computation.31 | convolution fusion | flops 4838129664 | bytes 14170112 | tf_op jit(solution)/shard_map/dot_general | solution.py:186
  438.9 9.7 %convolution_convert_fusion = bf16[768,3072]{1,0:T(8,128)(2,1)} fusion(bf16[1024,3072]{1,0:T(8,128)(2,1)} %get-tuple-element.103, f32[1024,768]{1,0:T(8,128)S(1)} %copy-done.7), kind=kOutput, calls=%fused_computation.30 | convolution fusion | flops 4834983936 | bytes 14155776 | tf_op jit(solution)/shard_map/dot_general | solution.py:186
  448.6 3.7 all-to-all-start.1
  453.6 88.5 %all-reduce.4.cloned.1.call-done = bf16[768,3,768]{2,1,0:T(4,128)(2,1)} async-done(((bf16[768,3,768]{2,1,0:T(4,128)(2,1)}), bf16[768,3,768]{2,1,0:T(4,128)(2,1)}) %all-reduce.4.cloned.1.call-update) | async-done | bytes 3538960
  543.1 12.4 %copy.39 = f32[48,3,768]{1,0,2:T(8,128)} copy(f32[48,3,768]{2,1,0:T(4,128)S(1)} %dynamic-slice_convert_fusion) | data formatting | bytes 884736
  555.5 13.0 %reshape.145 = f32[768,144]{1,0:T(8,128)} reshape(f32[768,48,3]{2,1,0:T(8,128)} %bitcast.78) | data formatting | bytes 884736
  568.5 19.1 %reduce-scatter.11.cloned.1.call-done = bf16[1024,768]{1,0:T(8,128)(2,1)} async-done(((bf16[2048,768]{1,0:T(8,128)(2,1)}), bf16[1024,768]{1,0:T(8,128)(2,1)}) %reduce-scatter.11.cloned.1.call-update) | async-done | bytes 1572880 | tf_op jit(solution)/shard_map/reduce_scatter | solution.py:308
  587.6 5.3 add_convert_fusion.2
  592.9 5.7 all-to-all-start.3
  598.7 55.5 %reduce-scatter.13.cloned.1.call-done = bf16[48,768]{1,0:T(8,128)(2,1)} async-done(((bf16[768,768]{1,0:T(8,128)(2,1)}), bf16[48,768]{1,0:T(8,128)(2,1)}) %reduce-scatter.13.cloned.1.call-update) | async-done | bytes 73744 | tf_op jit(solution)/shard_map/reduce_scatter | solution.py:234
  655.9 76.8 %reduce-scatter.17.cloned.1.call-done = bf16[48,3072]{1,0:T(8,128)(2,1)} async-done(((bf16[768,3072]{1,0:T(8,128)(2,1)}), bf16[48,3072]{1,0:T(8,128)(2,1)}) %reduce-scatter.17.cloned.1.call-update) | async-done | bytes 294928 | tf_op jit(solution)/shard_map/reduce_scatter | solution.py:234
  734.7 76.5 %reduce-scatter.21.cloned.1.call-done = bf16[48,3072]{1,0:T(8,128)(2,1)} async-done(((bf16[768,3072]{1,0:T(8,128)(2,1)}), bf16[48,3072]{1,0:T(8,128)(2,1)}) %reduce-scatter.21.cloned.1.call-update) | async-done | bytes 294928 | tf_op jit(solution)/shard_map/reduce_scatter | solution.py:234
  811.2 1.9 convert_element_type.118
  814.8 2.4 convert_reduce_fusion.1
  817.2 40.2 %psum.7 = f32[9216]{0:T(1024)S(1)} all-reduce(f32[9216]{0:T(1024)S(1)} %constant_dynamic-update-slice_fusion), channel_id=1, replica_groups=mesh['dp'=16,'tensor'=2] {'dp','tensor'}, use_global_device_ids=true, to_apply=%region_26.0 | all-reduce | flops 9216 | bytes 73728 | tf_op jit(solution)/shard_map/psum | solution.py:316
  859.4 7.3 reshape.146
  866.7 7.1 copy.38
  873.8 6.6 reduce-scatter.23.cloned.1.call-done
  (174 shorter events, 23.8 us)
Async XLA Ops:
  7.2 71.3 %copy-start.14 = (f32[48,384]{1,0:T(8,128)S(1)}, f32[48,384]{1,0:T(8,128)}, u32[]{:S(2)}) copy-start(f32[48,384]{1,0:T(8,128)} %param.21) | copy-start | bytes 221188
  7.2 76.2 %copy-start.12 = (f32[48,1536]{1,0:T(8,128)S(1)}, f32[48,1536]{1,0:T(8,128)}, u32[]{:S(2)}) copy-start(f32[48,1536]{1,0:T(8,128)} %param.22) | copy-start | bytes 884740
  7.2 121.2 %all-gather.8.cloned.1.call-start = ((), (), s32[]{:S(2)}) async-start(), calls=%async_computation.12 | async-start | bytes 3760128 | tf_op jit(solution)/shard_map/all_gather | solution.py:230
  15.1 124.8 %all-gather.10.cloned.1.call-start = ((), (), s32[]{:S(2)}) async-start(), calls=%async_computation.13 | async-start | bytes 4718592 | tf_op jit(solution)/shard_map/all_gather | solution.py:257
  78.3 16.3 %copy-start.13 = (f32[48,1536]{1,0:T(8,128)S(1)}, f32[48,1536]{1,0:T(8,128)}, u32[]{:S(2)}) copy-start(f32[48,1536]{1,0:T(8,128)} %param.23) | copy-start | bytes 884740
  78.4 27.3 %copy-start.35 = (s32[16]{0:T(128)S(1)}, s32[16]{0:T(128)}, u32[]{:S(2)}) copy-start(s32[16]{0:T(128)} %param.19) | copy-start | bytes 196
  78.4 29.2 %copy-start.27 = (f32[2,384]{1,0:T(2,128)S(1)}, f32[2,384]{1,0:T(2,128)}, u32[]{:S(2)}) copy-start(f32[2,384]{1,0:T(2,128)} %param.24) | copy-start | bytes 9220
  78.4 29.2 %copy-start.22 = (f32[1536]{0:T(1024)S(1)}, f32[1536]{0:T(1024)}, u32[]{:S(2)}) copy-start(f32[1536]{0:T(1024)} %param.26) | copy-start | bytes 18436
  78.4 34.7 %copy-start.36 = (s32[16]{0:T(128)S(1)}, s32[16]{0:T(128)}, u32[]{:S(2)}) copy-start(s32[16]{0:T(128)} %param.18) | copy-start | bytes 196
  78.4 48.0 %copy-start.15 = (f32[768]{0:T(1024)S(1)}, f32[768]{0:T(1024)}, u32[]{:S(2)}) copy-start(f32[768]{0:T(1024)} %param.30) | copy-start | bytes 9220
  78.4 119.9 %all-gather.12.cloned.1.call-start = ((), (), s32[]{:S(2)}) async-start(), calls=%async_computation.14 | async-start | bytes 1253376 | tf_op jit(solution)/shard_map/all_gather | solution.py:230
  83.3 139.4 %all-gather.14.cloned.1.call-start = ((), (), s32[]{:S(2)}) async-start(), calls=%async_computation.15 | async-start | bytes 5013504 | tf_op jit(solution)/shard_map/all_gather | solution.py:230
  90.3 36.1 %all-to-all-start.2 = ((bf16[16,64,768]{2,1,0:T(8,128)(2,1)}), bf16[16,64,768]{2,1,0:T(8,128)(2,1)S(1)}, u32[]{:S(2)}, u32[]{:S(2)}) async-start(bf16[16,64,768]{2,1,0:T(8,128)(2,1)} %bitcast.8), calls=%async_computation.2 | async-start | bytes 3145728 | tf_op jit(solution)/shard_map/all_to_all | solution.py:219
  94.6 182.0 %all-gather.16.cloned.1.call-start = ((), (), s32[]{:S(2)}) async-start(), calls=%async_computation.16 | async-start | bytes 5013504 | tf_op jit(solution)/shard_map/all_gather | solution.py:230
  105.6 436.5 %all-reduce.4.cloned.1.call-start = ((), (), s32[]{:S(2)}) async-start(), calls=%async_computation.25 | async-start | bytes 9437184
  126.4 5.3 copy-start
  131.7 4.4 copy-start.4
  149.1 49.2 %copy-start.31 = (f32[768]{0:T(1024)S(1)}, f32[768]{0:T(1024)}, u32[]{:S(2)}) copy-start(f32[768]{0:T(1024)} %param.25) | copy-start | bytes 9220
  202.1 113.6 %copy-start.2 = (f32[1024,768]{1,0:T(8,128)}, f32[1024,768]{1,0:T(8,128)S(1)}, u32[]{:S(2)}) copy-start(f32[1024,768]{1,0:T(8,128)S(1)} %get-tuple-element.102) | copy-start | bytes 9437188
  202.1 20.6 %copy-start.24 = (f32[768]{0:T(1024)S(1)}, f32[768]{0:T(1024)}, u32[]{:S(2)}) copy-start(f32[768]{0:T(1024)} %param.28) | copy-start | bytes 9220
  202.1 20.6 %copy-start.33 = (f32[768]{0:T(1024)S(1)}, f32[768]{0:T(1024)}, u32[]{:S(2)}) copy-start(f32[768]{0:T(1024)} %param.29) | copy-start | bytes 9220
  202.6 73.9 %copy-start.32 = (f32[768]{0:T(1024)S(1)}, f32[768]{0:T(1024)}, u32[]{:S(2)}) copy-start(f32[768]{0:T(1024)} %param.27) | copy-start | bytes 9220
  288.7 18.2 %slice-start = ((s8[4718592]{0:T(1024)(128)(4,1)}), s8[4194304]{0:T(1024)(128)(4,1)S(1)}, s32[]{:S(2)}) async-start(s8[4718592]{0:T(1024)(128)(4,1)} %bitcast.92), calls=%async_computation.26 | async-start | bytes 8388608
  291.8 15.1 %copy-start.6 = (f32[1024,768]{1,0:T(8,128)}, f32[1024,768]{1,0:T(8,128)S(1)}, u32[]{:S(2)}) copy-start(f32[1024,768]{1,0:T(8,128)S(1)} %get-tuple-element.91) | copy-start | bytes 9437188
  291.8 15.1 %slice-start.1 = ((s8[4718592]{0:T(1024)(128)(4,1)}), s8[524288]{0:T(1024)(128)(4,1)S(1)}, s32[]{:S(2)}) async-start(s8[4718592]{0:T(1024)(128)(4,1)} %bitcast.92), calls=%async_computation.27 | async-start | bytes 1048576
  319.6 76.2 %copy-start.5 = (bf16[16,64,768]{2,1,0:T(8,128)(2,1)S(1)}, bf16[16,64,768]{2,1,0:T(8,128)(2,1)}, u32[]{:S(2)}) copy-start(bf16[16,64,768]{2,1,0:T(8,128)(2,1)} %all_to_all.20) | copy-start | bytes 4718596
  395.8 3.3 copy-start.29
  410.9 5.2 copy-start.9
  410.9 176.7 %reduce-scatter.11.cloned.1.call-start = ((), (), s32[]{:S(2)}) async-start(), calls=%async_computation.17 | async-start | bytes 4718592 | tf_op jit(solution)/shard_map/reduce_scatter | solution.py:308
  421.5 5.3 copy-start.3
  421.5 5.3 copy-start.34
  421.5 232.7 %reduce-scatter.13.cloned.1.call-start = ((), (), s32[]{:S(2)}) async-start(), calls=%async_computation.18 | async-start | bytes 1253376 | tf_op jit(solution)/shard_map/reduce_scatter | solution.py:234
  426.8 305.9 %reduce-scatter.17.cloned.1.call-start = ((), (), s32[]{:S(2)}) async-start(), calls=%async_computation.20 | async-start | bytes 5013504 | tf_op jit(solution)/shard_map/reduce_scatter | solution.py:234
  437.0 374.2 %reduce-scatter.21.cloned.1.call-start = ((), (), s32[]{:S(2)}) async-start(), calls=%async_computation.22 | async-start | bytes 5013504 | tf_op jit(solution)/shard_map/reduce_scatter | solution.py:234
  448.6 3.8 copy-start.37
  448.6 144.3 %all-to-all-start.1 = ((bf16[16,64,768]{2,1,0:T(8,128)(2,1)}), bf16[16,64,768]{2,1,0:T(8,128)(2,1)S(1)}, u32[]{:S(2)}, u32[]{:S(2)}) async-start(bf16[16,64,768]{2,1,0:T(8,128)(2,1)} %bitcast.6), calls=%async_computation.1 | async-start | bytes 3145728 | tf_op jit(solution)/shard_map/all_to_all | solution.py:225
  452.3 407.1 %reduce-scatter.25.cloned.1.call-start = ((), (), s32[]{:S(2)}) async-start(), calls=%async_computation.24 | async-start | bytes 1179648
  555.5 32.1 %copy-start.11 = (bf16[1024,768]{1,0:T(8,128)(2,1)S(1)}, bf16[1024,768]{1,0:T(8,128)(2,1)}, u32[]{:S(2)}) copy-start(bf16[1024,768]{1,0:T(8,128)(2,1)} %get-tuple-element.21) | copy-start | bytes 4718596
  592.9 141.7 %copy-start.18 = (f32[768]{0:T(1024)S(1)}, f32[768]{0:T(1024)}, u32[]{:S(2)}) copy-start(f32[768]{0:T(1024)} %get-tuple-element.90) | copy-start | bytes 9220
  592.9 141.7 %copy-start.26 = (f32[768]{0:T(1024)S(1)}, f32[768]{0:T(1024)}, u32[]{:S(2)}) copy-start(f32[768]{0:T(1024)} %get-tuple-element.80) | copy-start | bytes 9220
  592.9 141.8 %copy-start.25 = (f32[768]{0:T(1024)S(1)}, f32[768]{0:T(1024)}, u32[]{:S(2)}) copy-start(f32[768]{0:T(1024)} %get-tuple-element.85) | copy-start | bytes 9220
  592.9 141.8 %copy-start.20 = (f32[768]{0:T(1024)S(1)}, f32[768]{0:T(1024)}, u32[]{:S(2)}) copy-start(f32[768]{0:T(1024)} %get-tuple-element.82) | copy-start | bytes 9220
  592.9 220.2 %copy-start.19 = (f32[768]{0:T(1024)S(1)}, f32[768]{0:T(1024)}, u32[]{:S(2)}) copy-start(f32[768]{0:T(1024)} %get-tuple-element.86) | copy-start | bytes 9220
  592.9 280.9 %all-to-all-start.3 = ((bf16[16,64,768]{2,1,0:T(8,128)(2,1)}), bf16[16,64,768]{2,1,0:T(8,128)(2,1)S(1)}, u32[]{:S(2)}, u32[]{:S(2)}) async-start(bf16[16,64,768]{2,1,0:T(8,128)(2,1)} %bitcast.88), calls=%async_computation.4 | async-start | bytes 3145728 | tf_op jit(solution)/shard_map/all_to_all | solution.py:225
  598.7 275.1 %reduce-scatter.15.cloned.1.call-start = ((), (), s32[]{:S(2)}) async-start(), calls=%async_computation.19 | async-start | bytes 221184 | tf_op jit(solution)/shard_map/reduce_scatter | solution.py:235
  655.8 218.0 %reduce-scatter.19.cloned.1.call-start = ((), (), s32[]{:S(2)}) async-start(), calls=%async_computation.21 | async-start | bytes 884736 | tf_op jit(solution)/shard_map/reduce_scatter | solution.py:235
  734.5 145.9 %reduce-scatter.23.cloned.1.call-start = ((), (), s32[]{:S(2)}) async-start(), calls=%async_computation.23 | async-start | bytes 884736 | tf_op jit(solution)/shard_map/reduce_scatter | solution.py:235
  734.6 82.6 %copy-start.21 = (f32[3072]{0:T(1024)S(1)}, f32[3072]{0:T(1024)}, u32[]{:S(2)}) copy-start(f32[3072]{0:T(1024)} %get-tuple-element.108) | copy-start | bytes 36868
  (10 other events, 22.9 us)
Sparse Core Ops, SparseCore 0:
  15.2 63.9 all-gather.7
  80.7 47.1 all-gather.9
  130.2 38.2 all-gather.11
  170.7 51.9 all-gather.13
  224.8 51.6 all-gather.15
  411.0 131.0 all-reduce.3
  544.3 43.1 reduce-scatter.10
  591.2 62.9 reduce-scatter.12
  658.1 74.5 reduce-scatter.16
  736.4 74.7 reduce-scatter.20
  813.4 17.1 reduce-scatter.24
  833.3 10.5 reduce-scatter.14
  846.7 15.7 reduce-scatter.18
  865.2 15.1 reduce-scatter.22

commit v2 on v1

--- a/solution.py
+++ b/solution.py
@@ -7,6 +7,7 @@
 from jax.experimental.pallas import tpu as pltpu
 from jax.sharding import PartitionSpec as P
 
+
 LOG2E = 1.4426950408889634
 MASKED = -1e30
 HEAD_DIM = 64
@@ -21,6 +22,11 @@
     return lax.broadcasted_iota(jnp.int32, shape, len(shape) - 1)
 
 
+def key_places(rows, start, total, place_ref):
+    spots = lax.broadcasted_iota(jnp.int32, (rows, PAIR), 0) + (start + place_ref[1])
+    return jnp.where(spots >= total, spots - total, spots)
+
+
 def attn_fwd_kernel(scale, len_ref, q_ref, k_ref, v_ref, o_ref, lse_ref, kx, vx):
     keys = k_ref.shape[0]
     rows = q_ref.shape[0]
@@ -28,7 +34,7 @@
     @pl.when(pl.program_id(1) == 0)
     def _():
         lanes = lane_iota((keys, PAIR))
-        valid = lax.broadcasted_iota(jnp.int32, (keys, PAIR), 0) < len_ref[0]
+        valid = key_places(keys, 0, keys, len_ref) < len_ref[0]
         bias = jnp.where(valid, 0.0, MASKED)
         k2 = k_ref[...].astype(jnp.float32)
         v2 = v_ref[...].astype(jnp.float32)
@@ -122,7 +128,7 @@
         dqt[...] = jnp.zeros_like(dqt)
 
     lanes = lane_iota((keys, PAIR))
-    valid = lax.broadcasted_iota(jnp.int32, (keys, PAIR), 0) + c * keys < len_ref[0]
+    valid = key_places(keys, c * keys, 2 * rows, len_ref) < len_ref[0]
     bias = jnp.where(valid, 0.0, MASKED)
     k2 = k_ref[...].astype(jnp.float32)
     v2 = v_ref[...].astype(jnp.float32)
@@ -225,16 +231,35 @@
     return lax.all_to_all(blocks, "dp", split_axis=0, concat_axis=0, tiled=True)[:, None]
 
 
-def gather_weight(weight):
-    low = lax.all_gather(weight.astype(jnp.bfloat16), "tensor", axis=weight.ndim - 1, tiled=True)
-    return lax.all_gather(low, "dp", axis=0, tiled=True)
-
-
-def scatter_weight(grad):
-    part = lax.psum_scatter(grad.astype(jnp.bfloat16), "dp", scatter_dimension=0, tiled=True)
-    return lax.psum_scatter(
-        part.astype(jnp.float32), "tensor", scatter_dimension=grad.ndim - 1, tiled=True
-    )
+def swap(value):
+    return lax.ppermute(value, "tensor", [(0, 1), (1, 0)])
+
+
+def in_order(own, other, axis):
+    first = lax.axis_index("tensor") == 0
+    return jnp.concatenate(
+        [jnp.where(first, own, other), jnp.where(first, other, own)], axis=axis
+    )
+
+
+def join(grads):
+    widths = [g.shape[1] // 2 for g in grads]
+    joined = jnp.concatenate([g.astype(jnp.bfloat16) for g in grads], axis=1)
+    return joined, widths
+
+
+def finish_sum(joined, widths):
+    part = lax.psum_scatter(joined, "dp", scatter_dimension=0, tiled=True)
+    part = part.astype(jnp.float32)
+    first = lax.axis_index("tensor") == 0
+    left, right, start = [], [], 0
+    for w in widths:
+        left.append(part[:, start : start + w])
+        right.append(part[:, start + w : start + 2 * w])
+        start += 2 * w
+    left = jnp.concatenate(left, axis=1)
+    right = jnp.concatenate(right, axis=1)
+    return jnp.where(first, left, right) + swap(jnp.where(first, right, left))
 
 
 def per_device(
@@ -244,26 +269,41 @@
     low = jnp.bfloat16
     tensor_index = lax.axis_index("tensor")
     width = x_in.shape[-1]
-    length = lengths[dealing[lax.axis_index("dp")]][None].astype(jnp.int32)
-    qkv_weight = gather_weight(w_qkv)
-    biases = lax.all_gather(
-        jnp.concatenate([b_qv.reshape(-1), b_in]), "tensor", axis=0, tiled=False
-    )
-    split = 2 * b_qv.shape[1]
-    qv_bias = biases[:, :split].reshape(-1, 2, b_qv.shape[1]).transpose(1, 0, 2).reshape(2, -1)
-    in_bias = biases[:, split:].reshape(-1)
+    length = lengths[dealing[lax.axis_index("dp")]].astype(jnp.int32)
+    shard = w_out.shape[0]
+    local = jnp.concatenate([w.reshape(shard, -1) for w in (w_qkv, w_out, w_in, w_ffo)], axis=1)
+    local = local.astype(low)
+    other = swap(local)
+    cuts = [0]
+    for w in (w_qkv[:, 0], w_qkv[:, 1], w_qkv[:, 2], w_out, w_in, w_ffo):
+        cuts.append(cuts[-1] + w.shape[1])
+    pieces = [in_order(local[:, i:j], other[:, i:j], 1) for i, j in zip(cuts[:-1], cuts[1:])]
+    qkv_weight = lax.all_gather(
+        jnp.concatenate(pieces[:3], axis=1), "dp", axis=0, tiled=True
+    )
+    late_weight = lax.all_gather(jnp.concatenate(pieces[3:], axis=1), "dp", axis=0, tiled=True)
+    hidden_width = 2 * w_in.shape[1]
+    out_weight = late_weight[:, :width]
+    in_weight = late_weight[:, width : width + hidden_width]
+    ffo_weight = late_weight[:, width + hidden_width :]
+    biases = jnp.concatenate([b_qv.reshape(-1), b_in])
+    other = swap(biases)
+    split = b_qv.shape[1]
+    qv_bias = [
+        in_order(biases[i * split : (i + 1) * split], other[i * split : (i + 1) * split], 0)
+        for i in range(2)
+    ]
+    in_bias = in_order(biases[2 * split :], other[2 * split :], 0)
     tokens_half = deal(x_in[:, 0])
     half_rows = tokens_half.shape[0]
-    tokens_full = lax.all_gather(tokens_half, "tensor", axis=0, tiled=True)
-    out_weight = gather_weight(w_out)
-    in_weight = gather_weight(w_in)
-    ffo_weight = gather_weight(w_ffo)
-    q_weight = qkv_weight[:, 0]
-    kv_weight = qkv_weight[:, 1:].reshape(width, -1)
+    tokens_full = jnp.concatenate([tokens_half, swap(tokens_half)], axis=0)
+    place = jnp.stack([length, tensor_index.astype(jnp.int32) * half_rows])
+    q_weight = qkv_weight[:, :width]
+    kv_weight = qkv_weight[:, width:]
     query = (dense(tokens_half, q_weight) + qv_bias[0]).astype(low)
     kv_bias = jnp.concatenate([jnp.zeros((width,), jnp.float32), qv_bias[1]])
     keyval = (dense(tokens_full, kv_weight) + kv_bias).astype(low)
-    mixed, totals = attn_fwd(length, query, keyval, 256)
+    mixed, totals = attn_fwd(place, query, keyval, 256)
     attn_half = contract_last(mixed, out_weight)
     first_norm, normed_one, inverse_one = norm_forward(
         tokens_half.astype(jnp.float32) + attn_half + b_out, ln1_gain, ln1_bias
@@ -280,9 +320,9 @@
     )
     ffo_bias_grad = jnp.sum(final_grad, axis=0)
     final_low = final_grad.astype(low)
-    ffo_sum = scatter_weight(contract_first(final_low, active))
+    ffo_part = contract_first(final_low, active)
     hidden_grad = (dense(final_low, ffo_weight) * gelu_slope(hidden)).astype(low)
-    in_sum = scatter_weight(contract_first(first_low, hidden_grad))
+    in_part = contract_first(first_low, hidden_grad)
     in_bias_grad = jnp.sum(hidden_grad.astype(jnp.float32), axis=0)
     first_grad = final_grad + contract_last(hidden_grad, in_weight)
     resid_grad, gain_one_grad, shift_one_grad = norm_backward(
@@ -290,23 +330,27 @@
     )
     out_bias_grad = jnp.sum(resid_grad, axis=0)
     resid_low = resid_grad.astype(low)
-    out_sum = scatter_weight(contract_first(resid_low, mixed))
+    late_part, widths = join([contract_first(resid_low, mixed), in_part, ffo_part])
     mixed_grad = dense(resid_low, out_weight).astype(low)
-    dq, dk, dv = attn_bwd(length, query, keyval, mixed, totals, mixed_grad, 512)
+    late_part, mixed_grad = lax.optimization_barrier((late_part, mixed_grad))
+    late_sum = finish_sum(late_part, widths)
+    out_sum, in_sum, ffo_sum = jnp.split(
+        late_sum, [w_out.shape[1], w_out.shape[1] + w_in.shape[1]], axis=1
+    )
+    dq, dk, dv = attn_bwd(place, query, keyval, mixed, totals, mixed_grad, 512)
     q_bias_grad = jnp.sum(dq.astype(jnp.float32), axis=0)
     v_bias_grad = jnp.sum(dv.astype(jnp.float32), axis=0)
-    qkv_grad = jnp.stack(
+    qkv_part, widths = join(
         [
             contract_first(tokens_half, dq),
             contract_first(tokens_full, dk),
             contract_first(tokens_full, dv),
-        ],
-        axis=1,
-    )
-    qkv_sum = scatter_weight(qkv_grad)
-    shared = contract_last(dk, qkv_weight[:, 1]) + contract_last(dv, qkv_weight[:, 2])
-    own = lax.psum_scatter(shared.astype(low), "tensor", scatter_dimension=0, tiled=True)
-    input_grad = resid_grad + contract_last(dq, q_weight) + own.astype(jnp.float32)
+        ]
+    )
+    qkv_sum = finish_sum(qkv_part, widths).reshape(w_qkv.shape)
+    shared = contract_last(dk, kv_weight[:, :width]) + contract_last(dv, kv_weight[:, width:])
+    own = shared[:half_rows] + swap(shared[half_rows:].astype(low)).astype(jnp.float32)
+    input_grad = resid_grad + contract_last(dq, q_weight) + own
     terms = jnp.concatenate(
         [
             out_bias_grad, ffo_bias_grad, gain_one_grad, shift_one_grad,
@@ -340,6 +384,7 @@
 
 def solution(mesh):
     tokens = P(None, "tensor", "dp", None)
+
     return jax.shard_map(
         per_device,
         mesh=mesh,

time: 898 us -> 666 us (0.74)
  waiting for transfers between devices: 373 us -> 177 us
  local copies, waits for them, and re-layouts: 63.3 us -> 29.2 us
  starting transfers between devices: 14.4 us -> 31.9 us
  matrix products: 139 us -> 123 us
  blocking collectives: 138 us -> 122 us
  other arithmetic: 20.2 us -> 30.7 us
    reduce_scatter x7 -> x1, waiting for transfers between devices: 234 us -> 72.3 us  [finish_sum(): part = lax.psum_scatter(joined, 'dp', scatter_dimension=0, tiled=True)]
    unnamed x16 -> x5, waiting for transfers between devices: 88.7 us -> 0.56 us
    ppermute x0 -> x6, waiting for transfers between devices: none -> 58.6 us  [swap(): return lax.ppermute(value, 'tensor', [(0, 1), (1, 0)])]
    all_gather x5 -> x2, waiting for transfers between devices: 36.7 us -> 0.01 us  [the longest x1 0.01 us: per_device(): lax.all_gather(jnp.concatenate(pieces[:3], axis=1), 'dp', axis=0, tiled=T...]
    all_gather x5 -> x0, blocking collectives: 34.2 us -> none  [the longest x4 29.5 us: gather_weight(): lax.all_gather(weight.astype(jnp.bfloat16), 'tensor', axis=weight.ndim -...]
    all_to_all x1, waiting for transfers between devices: 12.7 us -> 45.9 us  [deal(): out = lax.all_to_all(blocks, 'dp', split_axis=0, concat_axis=0, tiled=True)]
    unnamed x100 -> x92, local copies, waits for them, and re-layouts: 50.4 us -> 17.3 us
    psum x1, blocking collectives: 40.2 us -> 58.4 us  [per_device(): sums = lax.psum(terms, ('dp', 'tensor'))]
  transfers between devices with their start and end apart: 17 -> 13, of which waited for: 9 -> 5; matrix products, arithmetic and copies ran while one was open for 18% -> 7% of each run, Pallas kernels for 6% -> 8%
where the time goes in v2:
time: 666 us; the launch traced here: 657 us
  waiting for transfers between devices  177 us (27%)
  Pallas kernels  126 us (19%)
  matrix products  123 us (18%)
  blocking collectives  122 us (18%)
  starting transfers between devices  31.9 us (5%)
  other arithmetic  30.7 us (5%)
  local copies, waits for them, and re-layouts  29.2 us (4%)
  between operations  16.9 us (3%)
    pallas_call x1, Pallas kernels, attn_bwd(): pl.pallas_call(functools.partial(attn_bwd_kernel, LOG2E * HEAD_DIM ** (-0...  76.1 us
    reduce_scatter x1, waiting for transfers between devices, finish_sum(): part = lax.psum_scatter(joined, 'dp', scatter_dimension=0, tiled=True)  72.3 us
    dot_general x5, matrix products, dense(): return jnp.dot(a, b, preferred_element_type=jnp.float32)  63.4 us
    all_to_all x1, blocking collectives, deal(): out = lax.all_to_all(blocks, 'dp', split_axis=0, concat_axis=0, tiled=True)  63.3 us
    ppermute x6, waiting for transfers between devices, swap(): return lax.ppermute(value, 'tensor', [(0, 1), (1, 0)])  58.6 us
    psum x1, blocking collectives, per_device(): sums = lax.psum(terms, ('dp', 'tensor'))  58.4 us
    pallas_call x1, Pallas kernels, attn_fwd(): pl.pallas_call(functools.partial(attn_fwd_kernel, LOG2E * HEAD_DIM ** (-0...  50 us
    all_to_all x1, waiting for transfers between devices, deal(): out = lax.all_to_all(blocks, 'dp', split_axis=0, concat_axis=0, tiled=True)  45.9 us
  transfers between devices with their start and end apart: 13, of which 5 were waited for; matrix products, arithmetic and copies ran while one was open for 7% of the time, Pallas kernels for 8%

profile of v2, /device:TPU:0, one launch (start us, length us, event | category | flops | bytes accessed | tf_op | source)
XLA Modules:
  0.0 657.2 jit_solution(3357936674942378982)
XLA Ops:
  11.3 3.1 collective-permute-start
  14.4 10.2 %collective-permute-done = bf16[48,4608]{1,0:T(8,128)(2,1)S(1)} collective-permute-done((bf16[48,4608]{1,0:T(8,128)(2,1)S(1)}, bf16[48,4608]{1,0:T(8,128)(2,1)S(1)}, u32[]{:S(2)}, u32[]{:S(2)}) %collective-permute-start) | collective-permute-done | bytes 442400 | tf_op jit(solution)/shard_map/ppermute | solution.py:235
  27.5 63.3 %all_to_all.20 = bf16[16,64,768]{2,1,0:T(8,128)(2,1)} all-to-all(bf16[16,64,768]{2,1,0:T(8,128)(2,1)S(1)} %bitcast.60), channel_id=1, replica_groups=mesh['dp'=16,'tensor'=2] {'dp'}, dimensions={0} | all-to-all | bytes 3145728 | tf_op jit(solution)/shard_map/all_to_all | solution.py:225
  90.8 5.2 all-to-all-start.2
  96.1 1.6 collective-permute-start.1
  100.9 1.2 pad_add_fusion.len_ref
  102.7 45.9 %all-to-all-done.2 = bf16[16,64,768]{2,1,0:T(8,128)(2,1)S(1)} async-done(((bf16[16,64,768]{2,1,0:T(8,128)(2,1)}), bf16[16,64,768]{2,1,0:T(8,128)(2,1)S(1)}, u32[]{:S(2)}, u32[]{:S(2)}) %all-to-all-start.2) | async-done | bytes 1572896 | tf_op jit(solution)/shard_map/all_to_all | solution.py:225
  148.6 1.3 convert_reduce_fusion.2
  150.0 4.0 fusion.39.q_ref
  154.0 8.4 %add_convert_fusion.k_ref.v_ref = bf16[2048,1536]{1,0:T(8,128)(2,1)} fusion(f32[1536]{0:T(1024)S(1)} %pad_maximum_fusion.13, bf16[768,2304]{1,0:T(8,128)(2,1)S(1)} %copy-done.13, bf16[1024,768]{1,0:T(8,128)(2,1)} %collective-permute-done.2, bf16[1024,768]{1,0:T(8,128)(2,1)S(1)} %bitcast.64), kind=kOutput, calls=%fused_computation.25 | convolution fusion | flops 4844421120 | bytes 11804672 | tf_op jit(solution)/shard_map/dot_general | solution.py:196
  162.4 50.0 %attn_fwd.1 = (bf16[1024,768]{1,0:T(8,128)(2,1)}, f32[1024,768]{1,0:T(8,128)}) custom-call(s32[2]{0:T(128)} %pad_add_fusion.len_ref, bf16[1024,768]{1,0:T(8,128)(2,1)} %fusion.39.q_ref, bf16[2048,1536]{1,0:T(8,128)(2,1)} %add_convert_fusion.k_ref.v_ref, bf16[2048,1536]{1,0:T(8,128)(2,1)} %add_convert_fusion.k_ref.v_ref), custom_call_target="tpu_custom_call" | custom-call | flops 25769803776 | bytes 10000000 | tf_op jit(solution)/shard_map/attn_fwd/pallas_call | solution.py:70
  212.5 3.5 fusion.70
  217.4 34.5 %fusion.2 = (bf16[1024,3072]{1,0:T(8,128)(2,1)S(1)}, f32[1024,3072]{1,0:T(8,128)}) fusion(f32[3072]{0:T(1024)S(1)} %pad_maximum_fusion.12, bf16[768,6912]{1,0:T(8,128)(2,1)S(1)} %bitcast.72, f32[1024,768]{1,0:T(8,128)S(1)} %get-tuple-element.130, f32[768]{0:T(1024)S(1)} %copy-done.28, f32[768]{0:T(1024)S(1)} %copy-done.23, f32[1024]{0:T(1024)S(1)} %add_rsqrt_fusion.1, ...), kind=kOutput, calls=%fused_computation.4 | convolution fusion | flops 5043388416 | bytes 26767360 | tf_op jit(solution)/shard_map/dot_general | solution.py:196
  251.9 5.5 fusion.71
  257.9 1.8 fusion.31
  259.7 2.9 fusion.62
  262.6 6.9 %convolution_convert_fusion = bf16[768,3072]{1,0:T(8,128)(2,1)} fusion(bf16[1024,3072]{1,0:T(8,128)(2,1)S(1)} %bitcast.74, f32[1024,768]{1,0:T(8,128)S(1)} %get-tuple-element.95), kind=kOutput, calls=%fused_computation.30 | convolution fusion | flops 4834983936 | bytes 14155776 | tf_op jit(solution)/shard_map/dot_general | solution.py:192
  269.5 12.8 %convert_reduce_fusion = (f32[3072]{0:T(1024)S(1)}, bf16[1024,3072]{1,0:T(8,128)(2,1)S(1)}) fusion(f32[1024,3072]{1,0:T(8,128)} %get-tuple-element.132, f32[3072]{0:T(1024)S(1)} %pad_maximum_fusion.12, bf16[768,6912]{1,0:T(8,128)(2,1)S(1)} %bitcast.72, f32[1024,768]{1,0:T(8,128)S(1)} %get-tuple-element.95), kind=kOutput, calls=%fused_computation.11 | convolution fusion | flops 4873516032 | bytes 26763264 | tf_op jit(solution)/shard_map/dot_general | solution.py:196
  282.3 2.7 copy-done.31
  284.9 8.1 %convolution_convert_fusion.1 = bf16[768,3072]{1,0:T(8,128)(2,1)} fusion(bf16[1024,3072]{1,0:T(8,128)(2,1)S(1)} %get-tuple-element.137, f32[1024,768]{1,0:T(8,128)S(1)} %get-tuple-element.130, f32[768]{0:T(1024)S(1)} %copy-done.28, f32[768]{0:T(1024)S(1)} %copy-done.23, f32[1024]{0:T(1024)S(1)} %add_rsqrt_fusion.1, f32[1024]{0:T(1024)S(1)} %broadcast_multiply_fusion.5), kind=kOutput, calls=%fused_computation.31 | convolution fusion | flops 4838129664 | bytes 14170112 | tf_op jit(solution)/shard_map/dot_general | solution.py:192
  293.1 8.7 %multiply_reduce_fusion = (f32[768]{0:T(1024)}, f32[1024]{0:T(1024)S(1)}, f32[1024]{0:T(1024)S(1)}, f32[768]{0:T(1024)}, f32[1024,768]{1,0:T(8,128)S(1)}) fusion(f32[1024,768]{1,0:T(8,128)S(1)} %get-tuple-element.130, f32[1024]{0:T(1024)S(1)} %add_rsqrt_fusion.1, f32[1024]{0:T(1024)S(1)} %broadcast_multiply_fusion.5, f32[768]{0:T(1024)S(1)} %copy-done.23, ...), kind=kOutput, calls=%fused_computation.58 | convolution fusion | flops 4839698432 | bytes 20473856 | tf_op jit(solution)/shard_map/dot_general | solution.py:18
  303.2 2.5 convolution_convert_fusion.6
  305.7 2.4 copy.50
  308.1 9.2 %pad_maximum_fusion = bf16[768,6912]{1,0:T(8,128)(2,1)} fusion(bf16[768,3072]{1,0:T(8,128)(2,1)} %convolution_convert_fusion, bf16[768,3072]{1,0:T(8,128)(2,1)} %convolution_convert_fusion.1, bf16[768,768]{1,0:T(8,128)(2,1)} %copy.50), kind=kLoop, calls=%fused_computation.28 | loop fusion | flops 31850496 | bytes 21233664 | tf_op jit(solution)/shard_map/concatenate | solution.py:247
  317.2 3.8 convolution_convert_fusion.2.g_ref
  321.0 76.1 %attn_bwd.1 = (bf16[1024,768]{1,0:T(8,128)(2,1)}, bf16[2048,768]{1,0:T(8,128)(2,1)}, bf16[2048,768]{1,0:T(8,128)(2,1)}) custom-call(s32[2]{0:T(128)} %pad_add_fusion.len_ref, bf16[1024,768]{1,0:T(8,128)(2,1)} %fusion.39.q_ref, bf16[2048,1536]{1,0:T(8,128)(2,1)} %add_convert_fusion.k_ref.v_ref, bf16[2048,1536]{1,0:T(8,128)(2,1)} %add_convert_fusion.k_ref.v_ref, ...), custom_call_target="tpu_custom_call" | custom-call | flops 64424509440 | bytes 20000000 | tf_op jit(solution)/shard_map/attn_bwd/pallas_call | solution.py:170
  397.1 3.0 fusion.40
  400.2 4.3 convolution_convert_fusion.3
  404.5 4.1 convolution_convert_fusion.4
  409.0 4.0 copy.59
  413.6 10.4 %all-to-all-start.1 = ((bf16[16,64,768]{2,1,0:T(8,128)(2,1)}), bf16[16,64,768]{2,1,0:T(8,128)(2,1)}, u32[]{:S(2)}, u32[]{:S(2)}) async-start(bf16[16,64,768]{2,1,0:T(8,128)(2,1)} %bitcast.5), calls=%async_computation.1 | async-start | bytes 3145728 | tf_op jit(solution)/shard_map/all_to_all | solution.py:231
  424.1 4.9 fusion.42
  429.0 2.7 convolution_add_fusion
  431.7 2.6 copy-done.3
  434.3 1.3 slice.323
  435.6 1.5 collective-permute-start.3
  437.1 35.6 %collective-permute-done.3 = bf16[1024,768]{1,0:T(8,128)(2,1)} collective-permute-done((bf16[1024,768]{1,0:T(8,128)(2,1)}, bf16[1024,768]{1,0:T(8,128)(2,1)}, u32[]{:S(2)}, u32[]{:S(2)}) %collective-permute-start.3) | collective-permute-done | bytes 1572896 | tf_op jit(solution)/shard_map/ppermute | solution.py:235
  472.7 5.8 fusion.24
  478.6 5.8 all-to-all-start.3
  484.7 2.4 convert_reduce_fusion.1
  487.1 58.4 %psum.7 = f32[9216]{0:T(1024)S(1)} all-reduce(f32[9216]{0:T(1024)S(1)} %constant_dynamic-update-slice_fusion.6), channel_id=1, replica_groups=mesh['dp'=16,'tensor'=2] {'dp','tensor'}, use_global_device_ids=true, to_apply=%region_19.20 | all-reduce | flops 9216 | bytes 73728 | tf_op jit(solution)/shard_map/psum | solution.py:360
  546.8 1.3 copy.60
  549.6 2.3 collective-permute-start.4
  551.8 72.3 %reduce-scatter.5.cloned.1.call-done = bf16[48,6912]{1,0:T(8,128)(2,1)} async-done(((bf16[768,6912]{1,0:T(8,128)(2,1)}), bf16[48,6912]{1,0:T(8,128)(2,1)}) %reduce-scatter.5.cloned.1.call-update) | async-done | bytes 663568 | tf_op jit(solution)/shard_map/reduce_scatter | solution.py:252
  625.0 1.3 fusion.67
  627.1 1.5 collective-permute-start.5
  631.0 12.8 %collective-permute-done.5 = f32[48,3456]{1,0:T(8,128)} collective-permute-done((f32[48,3456]{1,0:T(8,128)}, f32[48,3456]{1,0:T(8,128)}, u32[]{:S(2)}, u32[]{:S(2)}) %collective-permute-start.5) | collective-permute-done | bytes 663584 | tf_op jit(solution)/shard_map/ppermute | solution.py:235
  646.4 2.7 copy.86
  (170 shorter events, 24.1 us)
Async XLA Ops:
  7.2 19.3 %copy-start.7 = (f32[48,1536]{1,0:T(8,128)S(1)}, f32[48,1536]{1,0:T(8,128)}, u32[]{:S(2)}) copy-start(f32[48,1536]{1,0:T(8,128)} %param.23) | copy-start | bytes 884740
  7.2 19.2 %copy-start.6 = (f32[48,1536]{1,0:T(8,128)S(1)}, f32[48,1536]{1,0:T(8,128)}, u32[]{:S(2)}) copy-start(f32[48,1536]{1,0:T(8,128)} %param.22) | copy-start | bytes 884740
  7.2 19.1 %copy-start.12 = (f32[48,384]{1,0:T(8,128)S(1)}, f32[48,384]{1,0:T(8,128)}, u32[]{:S(2)}) copy-start(f32[48,384]{1,0:T(8,128)} %param.21) | copy-start | bytes 221188
  7.2 142.8 %all-gather.3.cloned.1.call-start = ((), (), s32[]{:S(2)}) async-start(), calls=%async_computation.6 | async-start | bytes 3760128 | tf_op jit(solution)/shard_map/all_gather | solution.py:281
  8.3 19.2 %copy-start.8 = (bf16[16,1,64,768]{3,2,1,0:T(8,128)(2,1)S(1)}, bf16[16,1,64,768]{3,2,1,0:T(8,128)(2,1)}, u32[]{:S(2)}) copy-start(bf16[16,1,64,768]{3,2,1,0:T(8,128)(2,1)} %param.16) | copy-start | bytes 4718596
  11.3 13.2 %collective-permute-start = (bf16[48,4608]{1,0:T(8,128)(2,1)S(1)}, bf16[48,4608]{1,0:T(8,128)(2,1)S(1)}, u32[]{:S(2)}, u32[]{:S(2)}) collective-permute-start(bf16[48,4608]{1,0:T(8,128)(2,1)S(1)} %pad_maximum_fusion.8), channel_id=1, source_target_pairs={{0,1},{1,0},{2,3},{3,2},{4,5},{5,4},{6,7},{7,6},{8,9},{9,8},{10,11... | collective-permute-start | bytes 1327112 | tf_op jit(solution)/shard_map/ppermute | solution.py:235
  26.3 186.1 %all-gather.5.cloned.1.call-start = ((), (), s32[]{:S(2)}) async-start(), calls=%async_computation.7 | async-start | bytes 11280384 | tf_op jit(solution)/shard_map/all_gather | solution.py:284
  27.5 68.6 %copy-start.21 = (f32[2,384]{1,0:T(2,128)S(1)}, f32[2,384]{1,0:T(2,128)}, u32[]{:S(2)}) copy-start(f32[2,384]{1,0:T(2,128)} %param.24) | copy-start | bytes 9220
  27.5 68.6 %copy-start.17 = (f32[1536]{0:T(1024)S(1)}, f32[1536]{0:T(1024)}, u32[]{:S(2)}) copy-start(f32[1536]{0:T(1024)} %param.26) | copy-start | bytes 18436
  27.5 70.2 %copy-start.29 = (s32[16]{0:T(128)S(1)}, s32[16]{0:T(128)}, u32[]{:S(2)}) copy-start(s32[16]{0:T(128)} %param.19) | copy-start | bytes 196
  27.5 72.8 %copy-start.30 = (s32[16]{0:T(128)S(1)}, s32[16]{0:T(128)}, u32[]{:S(2)}) copy-start(s32[16]{0:T(128)} %param.18) | copy-start | bytes 196
  27.5 121.1 %copy-start.16 = (f32[768]{0:T(1024)S(1)}, f32[768]{0:T(1024)}, u32[]{:S(2)}) copy-start(f32[768]{0:T(1024)} %param.30) | copy-start | bytes 9220
  90.8 11.3 %copy-start.9 = (bf16[16,64,768]{2,1,0:T(8,128)(2,1)S(1)}, bf16[16,64,768]{2,1,0:T(8,128)(2,1)}, u32[]{:S(2)}) copy-start(bf16[16,64,768]{2,1,0:T(8,128)(2,1)} %all_to_all.20) | copy-start | bytes 4718596
  90.8 57.7 %all-to-all-start.2 = ((bf16[16,64,768]{2,1,0:T(8,128)(2,1)}), bf16[16,64,768]{2,1,0:T(8,128)(2,1)S(1)}, u32[]{:S(2)}, u32[]{:S(2)}) async-start(bf16[16,64,768]{2,1,0:T(8,128)(2,1)} %bitcast.61), calls=%async_computation.2 | async-start | bytes 3145728 | tf_op jit(solution)/shard_map/all_to_all | solution.py:225
  96.0 450.8 %reduce-scatter.7.cloned.1.call-start = ((), (), s32[]{:S(2)}) async-start(), calls=%async_computation.9 | async-start | bytes 3760128
  96.1 6.5 collective-permute-start.1
  102.1 51.9 %collective-permute-start.2 = (bf16[1024,768]{1,0:T(8,128)(2,1)S(1)}, bf16[1024,768]{1,0:T(8,128)(2,1)}, u32[]{:S(2)}, u32[]{:S(2)}) collective-permute-start(bf16[1024,768]{1,0:T(8,128)(2,1)S(1)} %bitcast.62), channel_id=1, source_target_pairs={{0,1},{1,0},{2,3},{3,2},{4,5},{5,4},{6,7},{7,6},{8,9},{9,8},{10,11... | collective-permute-start | bytes 4718600 | tf_op jit(solution)/shard_map/ppermute | solution.py:235
  150.0 4.0 copy-start.13
  162.4 50.0 %copy-start.26 = (f32[768]{0:T(1024)S(1)}, f32[768]{0:T(1024)}, u32[]{:S(2)}) copy-start(f32[768]{0:T(1024)} %param.25) | copy-start | bytes 9220
  212.4 4.1 slice-start
  212.4 4.3 slice-start.1
  212.5 4.9 slice-start.2
  217.4 34.5 %copy-start.27 = (f32[768]{0:T(1024)S(1)}, f32[768]{0:T(1024)}, u32[]{:S(2)}) copy-start(f32[768]{0:T(1024)} %param.27) | copy-start | bytes 9220
  251.9 5.5 copy-start.32
  257.9 1.8 copy-start.22
  257.9 4.7 slice-start.3
  259.7 2.9 slice-start.4
  282.3 2.7 copy-start.31
  302.9 14.4 %copy-start = (f32[1024,768]{1,0:T(8,128)}, f32[1024,768]{1,0:T(8,128)S(1)}, u32[]{:S(2)}) copy-start(f32[1024,768]{1,0:T(8,128)S(1)} %get-tuple-element.97) | copy-start | bytes 9437188
  321.0 76.1 %copy-start.10 = (bf16[16,64,768]{2,1,0:T(8,128)(2,1)S(1)}, bf16[16,64,768]{2,1,0:T(8,128)(2,1)}, u32[]{:S(2)}) copy-start(bf16[16,64,768]{2,1,0:T(8,128)(2,1)} %all_to_all.20) | copy-start | bytes 4718596
  397.1 3.0 copy-start.4
  400.1 4.3 copy-start.33
  413.1 211.1 %reduce-scatter.5.cloned.1.call-start = ((), (), s32[]{:S(2)}) async-start(), calls=%async_computation.8 | async-start | bytes 11280384 | tf_op jit(solution)/shard_map/reduce_scatter | solution.py:252
  413.1 11.0 %copy-start.14 = (bf16[768,2304]{1,0:T(8,128)(2,1)S(1)}, bf16[768,2304]{1,0:T(8,128)(2,1)}, u32[]{:S(2)}) copy-start(bf16[768,2304]{1,0:T(8,128)(2,1)} %all-gather.3.cloned.1.call-done) | copy-start | bytes 10616836
  413.6 64.9 %all-to-all-start.1 = ((bf16[16,64,768]{2,1,0:T(8,128)(2,1)}), bf16[16,64,768]{2,1,0:T(8,128)(2,1)}, u32[]{:S(2)}, u32[]{:S(2)}) async-start(bf16[16,64,768]{2,1,0:T(8,128)(2,1)} %bitcast.5), calls=%async_computation.1 | async-start | bytes 3145728 | tf_op jit(solution)/shard_map/all_to_all | solution.py:231
  424.1 4.9 copy-start.5
  431.7 2.6 copy-start.3
  434.3 2.8 copy-start.18
  434.3 2.8 copy-start.25
  434.3 2.8 copy-start.24
  434.3 38.5 %copy-start.1 = (f32[1024,768]{1,0:T(8,128)S(1)}, f32[1024,768]{1,0:T(8,128)}, u32[]{:S(2)}) copy-start(f32[1024,768]{1,0:T(8,128)} %copy-done) | copy-start | bytes 9437188
  435.6 37.2 %collective-permute-start.3 = (bf16[1024,768]{1,0:T(8,128)(2,1)}, bf16[1024,768]{1,0:T(8,128)(2,1)}, u32[]{:S(2)}, u32[]{:S(2)}) collective-permute-start(bf16[1024,768]{1,0:T(8,128)(2,1)} %slice.323), channel_id=1, source_target_pairs={{0,1},{1,0},{2,3},{3,2},{4,5},{5,4},{6,7},{7,6},{8,9},{9,8},{10,11... | collective-permute-start | bytes 4718600 | tf_op jit(solution)/shard_map/ppermute | solution.py:235
  478.5 5.8 copy-start.20
  478.5 5.8 copy-start.19
  478.5 5.9 copy-start.2
  478.6 150.7 %all-to-all-start.3 = ((bf16[16,64,768]{2,1,0:T(8,128)(2,1)}), bf16[16,64,768]{2,1,0:T(8,128)(2,1)S(1)}, u32[]{:S(2)}, u32[]{:S(2)}) async-start(bf16[16,64,768]{2,1,0:T(8,128)(2,1)} %bitcast.52), calls=%async_computation.3 | async-start | bytes 3145728 | tf_op jit(solution)/shard_map/all_to_all | solution.py:231
  549.6 79.7 %collective-permute-start.4 = (f32[48,1152]{1,0:T(8,128)}, f32[48,1152]{1,0:T(8,128)}, u32[]{:S(2)}, u32[]{:S(2)}) collective-permute-start(f32[48,1152]{1,0:T(8,128)} %fusion.56), channel_id=1, source_target_pairs={{0,1},{1,0},{2,3},{3,2},{4,5},{5,4},{6,7},{7,6},{8,9},{9,8},{10,11... | collective-permute-start | bytes 663560 | tf_op jit(solution)/shard_map/ppermute | solution.py:235
  627.1 16.6 %collective-permute-start.5 = (f32[48,3456]{1,0:T(8,128)}, f32[48,3456]{1,0:T(8,128)}, u32[]{:S(2)}, u32[]{:S(2)}) collective-permute-start(f32[48,3456]{1,0:T(8,128)} %fusion.55), channel_id=1, source_target_pairs={{0,1},{1,0},{2,3},{3,2},{4,5},{5,4},{6,7},{7,6},{8,9},{9,8},{10,11... | collective-permute-start | bytes 1990664 | tf_op jit(solution)/shard_map/ppermute | solution.py:235
  (5 other events, 5.9 us)
Sparse Core Ops, SparseCore 0:
  26.4 64.8 all-gather.2
  93.6 113.4 all-gather.4
  413.2 89.0 reduce-scatter.6
  506.2 117.8 reduce-scatter.4

commit v3 on v2

--- a/solution.py
+++ b/solution.py
@@ -221,6 +221,218 @@
     )
 
 
+def mesh_copy(src, dst, send_sem, recv_sem, dp, tensor):
+    return pltpu.make_async_remote_copy(
+        src_ref=src,
+        dst_ref=dst,
+        send_sem=send_sem,
+        recv_sem=recv_sem,
+        device_id={"dp": dp, "tensor": tensor},
+        device_id_type=pl.DeviceIdType.MESH,
+    )
+
+
+def greet_all(n, me, side):
+    barrier = pltpu.get_barrier_semaphore()
+
+    def greet(step, carry):
+        pl.semaphore_signal(
+            barrier,
+            inc=1,
+            device_id={"dp": lax.rem(me + step, n), "tensor": side},
+            device_id_type=pl.DeviceIdType.MESH,
+        )
+        return carry
+
+    lax.fori_loop(1, n, greet, 0)
+    pl.semaphore_signal(
+        barrier,
+        inc=1,
+        device_id={"dp": me, "tensor": 1 - side},
+        device_id_type=pl.DeviceIdType.MESH,
+    )
+    pl.semaphore_wait(barrier, n)
+
+
+def repeat(low, high, body):
+    def step_body(step, carry):
+        body(step)
+        return carry
+
+    lax.fori_loop(low, high, step_body, 0)
+
+
+def deal_kernel(n, x_ref, o_ref, send, recv, relay_send, relay_recv):
+    me, side = lax.axis_index("dp"), lax.axis_index("tensor")
+    greet_all(n, me, side)
+
+    def direct(step):
+        dest = lax.rem(me + step, n)
+        return mesh_copy(
+            x_ref.at[dest], o_ref.at[0, me], send.at[step], recv.at[step], dest, side
+        )
+
+    def arrival(step):
+        src = lax.rem(me + n - step, n)
+        return mesh_copy(
+            x_ref.at[src], o_ref.at[0, src], send.at[step], recv.at[step], src, side
+        )
+
+    def relay(step):
+        src = lax.rem(me + n - step, n)
+        return mesh_copy(
+            o_ref.at[0, src], o_ref.at[1, src], relay_send.at[step], relay_recv.at[step],
+            me, 1 - side,
+        )
+
+    repeat(1, n, lambda step: direct(step).start())
+    first = mesh_copy(
+        x_ref.at[me], o_ref.at[1, me], relay_send.at[0], relay_recv.at[0], me, 1 - side
+    )
+    first.start()
+    o_ref[0, me] = x_ref[me]
+
+    def pass_on(step):
+        arrival(step).wait_recv()
+        relay(step).start()
+
+    repeat(1, n, pass_on)
+
+    def finish(step):
+        direct(step).wait_send()
+        relay(step).wait()
+
+    repeat(1, n, finish)
+    first.wait()
+
+
+def deal_both(blocks):
+    n, rows, width = blocks.shape
+    vmem = pl.BlockSpec(memory_space=pltpu.VMEM)
+    out = pl.pallas_call(
+        functools.partial(deal_kernel, n),
+        out_shape=jax.ShapeDtypeStruct((2, n, rows, width), blocks.dtype),
+        in_specs=[vmem],
+        out_specs=vmem,
+        scratch_shapes=[pltpu.SemaphoreType.DMA((n,))] * 4,
+        compiler_params=pltpu.CompilerParams(collective_id=0, has_side_effects=True),
+        name="deal_both",
+    )(blocks)
+    return out.reshape(2 * n * rows, width)
+
+
+def settle_kernel(
+    n, own_ref, far_ref, terms_ref, out_ref, sums_ref, inbox, stage, their, pair, pile, total,
+    a_send, a_recv, y_send, y_recv, b_send, b_recv, c_send, c_recv, d_send, d_recv,
+):
+    me, side = lax.axis_index("dp"), lax.axis_index("tensor")
+    greet_all(n, me, side)
+    whole = mesh_copy(terms_ref, their, a_send, a_recv, me, 1 - side)
+    whole.start()
+
+    def across(step):
+        dest = lax.rem(me + step, n)
+        return mesh_copy(
+            far_ref.at[dest], inbox.at[dest], y_send.at[step], y_recv.at[step], me, 1 - side
+        )
+
+    def home(step, src_side):
+        dest = lax.rem(me + step, n)
+        src = lax.rem(me + n - step, n)
+        where = src if src_side else me
+        return mesh_copy(
+            stage.at[dest], out_ref.at[where], d_send.at[step], d_recv.at[step], dest, side
+        )
+
+    def chunk(step, src_side):
+        dest = lax.rem(me + step, n)
+        src = lax.rem(me + n - step, n)
+        where = src if src_side else me
+        return mesh_copy(
+            pair.at[dest], pile.at[where], b_send.at[step], b_recv.at[step], dest, side
+        )
+
+    def share(step, src_side):
+        dest = lax.rem(me + step, n)
+        src = lax.rem(me + n - step, n)
+        where = src if src_side else me
+        return mesh_copy(
+            total, sums_ref.at[where], c_send.at[step], c_recv.at[step], dest, side
+        )
+
+    repeat(1, n, lambda step: across(step).start())
+    across(0).start()
+    whole.wait()
+    pair[...] = terms_ref[...] + their[...]
+    pile[me] = pair[me]
+
+    def add(step):
+        across(step).wait_recv()
+        dest = lax.rem(me + step, n)
+        stage[dest] = (own_ref[dest] + inbox[dest].astype(jnp.float32)).astype(stage.dtype)
+
+    add(1)
+    repeat(1, n, lambda step: chunk(step, False).start())
+
+    def move(step):
+        add(step)
+        home(step - 1, False).start()
+
+    repeat(2, n, move)
+    across(0).wait_recv()
+    out_ref[me] = (own_ref[me] + inbox[me].astype(jnp.float32)).astype(out_ref.dtype)
+    home(n - 1, False).start()
+    repeat(1, n, lambda step: chunk(step, True).wait_recv())
+    total[...] = jnp.sum(pile[...], axis=0)
+    sums_ref[me] = total[...]
+    repeat(1, n, lambda step: home(step, True).wait_recv())
+    repeat(1, n, lambda step: share(step, False).start())
+
+    def finish(step):
+        share(step, True).wait_recv()
+        share(step, False).wait_send()
+        home(step, False).wait_send()
+        chunk(step, False).wait_send()
+        across(step).wait_send()
+
+    repeat(1, n, finish)
+    across(0).wait_send()
+
+
+def settle(own, far, terms):
+    n = lax.axis_size("dp")
+    rows, width = own.shape
+    per = rows // n
+    lines = 8 * -(-terms.shape[0] // (n * 1024))
+    padded = jnp.pad(terms, (0, n * lines * 128 - terms.shape[0])).reshape(n, lines, 128)
+    vmem = pl.BlockSpec(memory_space=pltpu.VMEM)
+    low = jnp.bfloat16
+    blocks = (n, per, width)
+    out, sums = pl.pallas_call(
+        functools.partial(settle_kernel, n),
+        out_shape=[
+            jax.ShapeDtypeStruct(blocks, low),
+            jax.ShapeDtypeStruct(padded.shape, jnp.float32),
+        ],
+        in_specs=[vmem] * 3,
+        out_specs=[vmem] * 2,
+        scratch_shapes=[
+            pltpu.VMEM(blocks, low),
+            pltpu.VMEM(blocks, low),
+            pltpu.VMEM(padded.shape, jnp.float32),
+            pltpu.VMEM(padded.shape, jnp.float32),
+            pltpu.VMEM(padded.shape, jnp.float32),
+            pltpu.VMEM((lines, 128), jnp.float32),
+            pltpu.SemaphoreType.DMA,
+            pltpu.SemaphoreType.DMA,
+        ]
+        + [pltpu.SemaphoreType.DMA((n,))] * 8,
+        compiler_params=pltpu.CompilerParams(collective_id=1, has_side_effects=True),
+        name="settle",
+    )(own.reshape(blocks), far.reshape(blocks), padded)
+    return out[:, None], sums.reshape(-1)[: terms.shape[0]]
+
+
 def deal(blocks):
     out = lax.all_to_all(blocks, "dp", split_axis=0, concat_axis=0, tiled=True)
     return out.reshape(-1, out.shape[-1])
@@ -270,18 +482,20 @@
     tensor_index = lax.axis_index("tensor")
     width = x_in.shape[-1]
     length = lengths[dealing[lax.axis_index("dp")]].astype(jnp.int32)
-    shard = w_out.shape[0]
-    local = jnp.concatenate([w.reshape(shard, -1) for w in (w_qkv, w_out, w_in, w_ffo)], axis=1)
-    local = local.astype(low)
-    other = swap(local)
-    cuts = [0]
-    for w in (w_qkv[:, 0], w_qkv[:, 1], w_qkv[:, 2], w_out, w_in, w_ffo):
-        cuts.append(cuts[-1] + w.shape[1])
-    pieces = [in_order(local[:, i:j], other[:, i:j], 1) for i, j in zip(cuts[:-1], cuts[1:])]
+
+    def paired(weights):
+        local = jnp.concatenate([w.astype(low) for w in weights], axis=1)
+        other = swap(local)
+        cuts = [0]
+        for w in weights:
+            cuts.append(cuts[-1] + w.shape[1])
+        pieces = [in_order(local[:, i:j], other[:, i:j], 1) for i, j in zip(cuts[:-1], cuts[1:])]
+        return jnp.concatenate(pieces, axis=1)
+
     qkv_weight = lax.all_gather(
-        jnp.concatenate(pieces[:3], axis=1), "dp", axis=0, tiled=True
-    )
-    late_weight = lax.all_gather(jnp.concatenate(pieces[3:], axis=1), "dp", axis=0, tiled=True)
+        paired([w_qkv[:, 0], w_qkv[:, 1], w_qkv[:, 2]]), "dp", axis=0, tiled=True
+    )
+    late_weight = lax.all_gather(paired([w_out, w_in, w_ffo]), "dp", axis=0, tiled=True)
     hidden_width = 2 * w_in.shape[1]
     out_weight = late_weight[:, :width]
     in_weight = late_weight[:, width : width + hidden_width]
@@ -294,9 +508,11 @@
         for i in range(2)
     ]
     in_bias = in_order(biases[2 * split :], other[2 * split :], 0)
-    tokens_half = deal(x_in[:, 0])
-    half_rows = tokens_half.shape[0]
-    tokens_full = jnp.concatenate([tokens_half, swap(tokens_half)], axis=0)
+    tokens_full = deal_both(x_in[:, 0])
+    half_rows = tokens_full.shape[0] // 2
+    tokens_half = tokens_full[:half_rows]
+    tokens_full, cotangent = lax.optimization_barrier((tokens_full, cotangent))
+    output_grad = deal(cotangent[:, 0]).astype(jnp.float32)
     place = jnp.stack([length, tensor_index.astype(jnp.int32) * half_rows])
     q_weight = qkv_weight[:, :width]
     kv_weight = qkv_weight[:, width:]
@@ -314,7 +530,6 @@
     result, normed_two, inverse_two = norm_forward(
         first_norm + contract_last(active, ffo_weight) + b_ffo, ln2_gain, ln2_bias
     )
-    output_grad = deal(cotangent[:, 0]).astype(jnp.float32)
     final_grad, gain_two_grad, shift_two_grad = norm_backward(
         output_grad, normed_two, inverse_two, ln2_gain
     )
@@ -349,24 +564,24 @@
     )
     qkv_sum = finish_sum(qkv_part, widths).reshape(w_qkv.shape)
     shared = contract_last(dk, kv_weight[:, :width]) + contract_last(dv, kv_weight[:, width:])
-    own = shared[:half_rows] + swap(shared[half_rows:].astype(low)).astype(jnp.float32)
-    input_grad = resid_grad + contract_last(dq, q_weight) + own
+    own = resid_grad + contract_last(dq, q_weight) + shared[:half_rows]
     terms = jnp.concatenate(
         [
             out_bias_grad, ffo_bias_grad, gain_one_grad, shift_one_grad,
             gain_two_grad, shift_two_grad, q_bias_grad, v_bias_grad, in_bias_grad,
         ]
     )
-    sums = lax.psum(terms, ("dp", "tensor"))
+    input_grad, sums = settle(own, shared[half_rows:].astype(low), terms)
     norm_sums = sums[: 6 * width].reshape(6, width)
     qv_sums = sums[6 * width : 8 * width].reshape(2, width)
     share = b_qv.shape[1]
     qv_share = lax.dynamic_slice_in_dim(qv_sums, tensor_index * share, share, 1)
     share = b_in.shape[0]
     in_share = lax.dynamic_slice_in_dim(sums[8 * width :], tensor_index * share, share, 0)
+    output = undeal(result.astype(low))
     return (
-        undeal(result.astype(low)),
-        undeal(input_grad.astype(low)),
+        output,
+        input_grad,
         qkv_sum,
         out_sum,
         in_sum,

time: 666 us -> 695 us (1.044)
  Pallas kernels: 126 us -> 267 us
  blocking collectives: 122 us -> 0 us
  starting transfers between devices: 31.9 us -> 58.1 us
  waiting for transfers between devices: 177 us -> 169 us
    pallas_call x0 -> x2, Pallas kernels: none -> 141 us  [the longest x1 85.1 us: settle(): pl.pallas_call(functools.partial(settle_kernel, n), out_shape=[jax.ShapeD...]
    all_to_all x1 -> x0, blocking collectives: 63.3 us -> none  [deal(): out = lax.all_to_all(blocks, 'dp', split_axis=0, concat_axis=0, tiled=True)]
    psum x1 -> x0, blocking collectives: 58.4 us -> none  [per_device(): sums = lax.psum(terms, ('dp', 'tensor'))]
    reduce_scatter x1, waiting for transfers between devices: 72.3 us -> 110 us  [finish_sum(): part = lax.psum_scatter(joined, 'dp', scatter_dimension=0, tiled=True)]
    ppermute x6 -> x5, waiting for transfers between devices: 58.6 us -> 23.1 us  [swap(): return lax.ppermute(value, 'tensor', [(0, 1), (1, 0)])]
    all_to_all x1, starting transfers between devices: 5.17 us -> 24.2 us  [deal(): out = lax.all_to_all(blocks, 'dp', split_axis=0, concat_axis=0, tiled=True)]
    all_to_all x1, waiting for transfers between devices: 45.9 us -> 35.5 us  [deal(): out = lax.all_to_all(blocks, 'dp', split_axis=0, concat_axis=0, tiled=True)]
    all_to_all x2 -> x1, starting transfers between devices: 16.2 us -> 24.9 us  [undeal(): lax.all_to_all(blocks, 'dp', split_axis=0, concat_axis=0, tiled=True)]
  transfers between devices with their start and end apart: 13 -> 11, of which waited for: 5 -> 5; matrix products, arithmetic and copies ran while one was open for 7% -> 7% of each run, Pallas kernels for 8% -> 28%
where the time goes in v3:
time: 695 us; the launch traced here: 686 us
  Pallas kernels  267 us (38%)
  waiting for transfers between devices  169 us (24%)
  matrix products  117 us (17%)
  starting transfers between devices  58.1 us (8%)
  other arithmetic  28.9 us (4%)
  local copies, waits for them, and re-layouts  28.6 us (4%)
  between operations  17 us (2%)
    reduce_scatter x1, waiting for transfers between devices, finish_sum(): part = lax.psum_scatter(joined, 'dp', scatter_dimension=0, tiled=True)  110 us
    pallas_call x1, Pallas kernels, settle(): pl.pallas_call(functools.partial(settle_kernel, n), out_shape=[jax.ShapeD...  85.1 us
    pallas_call x1, Pallas kernels, attn_bwd(): pl.pallas_call(functools.partial(attn_bwd_kernel, LOG2E * HEAD_DIM ** (-0...  76.2 us
    dot_general x5, matrix products, dense(): return jnp.dot(a, b, preferred_element_type=jnp.float32)  62.7 us
    pallas_call x1, Pallas kernels, deal_both(): pl.pallas_call(functools.partial(deal_kernel, n), out_shape=jax.ShapeDtyp...  55.4 us
    pallas_call x1, Pallas kernels, attn_fwd(): pl.pallas_call(functools.partial(attn_fwd_kernel, LOG2E * HEAD_DIM ** (-0...  50 us
    all_to_all x1, waiting for transfers between devices, deal(): out = lax.all_to_all(blocks, 'dp', split_axis=0, concat_axis=0, tiled=True)  35.5 us
    dot_general x6, matrix products, contract_last(): lax.dot_general(a, b, (((1,), (1,)), ((), ())), preferred_element_type=jn...  28.4 us
  transfers between devices with their start and end apart: 11, of which 5 were waited for; matrix products, arithmetic and copies ran while one was open for 7% of the time, Pallas kernels for 28%

profile of v3, /device:TPU:0, one launch (start us, length us, event | category | flops | bytes accessed | tf_op | source)
XLA Modules:
  0.0 686.2 jit_solution(17388165893705921757)
XLA Ops:
  8.3 3.1 collective-permute-start
  11.4 3.1 collective-permute-done
  18.2 1.8 collective-permute-start.2
  20.0 7.2 %collective-permute-done.2 = bf16[48,3456]{1,0:T(8,128)(2,1)S(1)} collective-permute-done((bf16[48,3456]{1,0:T(8,128)(2,1)S(1)}, bf16[48,3456]{1,0:T(8,128)(2,1)S(1)}, u32[]{:S(2)}, u32[]{:S(2)}) %collective-permute-start.2) | collective-permute-done | bytes 331808 | tf_op jit(solution)/shard_map/ppermute | solution.py:447
  28.4 55.4 %deal_both.1 = bf16[2,16,64,768]{3,2,1,0:T(8,128)(2,1)} custom-call(bf16[16,64,768]{2,1,0:T(8,128)(2,1)} %bitcast.89), custom_call_target="tpu_custom_call" | custom-call | tf_op jit(solution)/shard_map/deal_both/pallas_call | solution.py:312
  83.8 24.2 %all-to-all-start.1 = ((bf16[16,64,768]{2,1,0:T(8,128)(2,1)}), bf16[16,64,768]{2,1,0:T(8,128)(2,1)S(1)}, u32[]{:S(2)}, u32[]{:S(2)}) async-start(bf16[16,64,768]{2,1,0:T(8,128)(2,1)} %bitcast.11), calls=%async_computation.1 | async-start | bytes 3145728 | tf_op jit(solution)/shard_map/all_to_all | solution.py:437
  111.9 1.2 pad_add_fusion.len_ref
  113.2 1.5 slice.173
  114.8 35.5 %all-to-all-done.1 = bf16[16,64,768]{2,1,0:T(8,128)(2,1)S(1)} async-done(((bf16[16,64,768]{2,1,0:T(8,128)(2,1)}), bf16[16,64,768]{2,1,0:T(8,128)(2,1)S(1)}, u32[]{:S(2)}, u32[]{:S(2)}) %all-to-all-start.1) | async-done | bytes 1572896 | tf_op jit(solution)/shard_map/all_to_all | solution.py:437
  150.3 1.3 convert_reduce_fusion.2
  151.7 4.0 fusion.40.q_ref
  155.7 7.1 %add_convert_fusion.k_ref.v_ref = bf16[2048,1536]{1,0:T(8,128)(2,1)} fusion(f32[1536]{0:T(1024)S(1)} %pad_maximum_fusion.10, bf16[2048,768]{1,0:T(8,128)(2,1)S(1)} %bitcast.80, bf16[768,2304]{1,0:T(8,128)(2,1)S(1)} %copy-done.14), kind=kOutput, calls=%fused_computation.25 | convolution fusion | flops 4838129664 | bytes 11804672 | tf_op jit(solution)/shard_map/dot_general | solution.py:196
  162.8 50.0 %attn_fwd.1 = (bf16[1024,768]{1,0:T(8,128)(2,1)}, f32[1024,768]{1,0:T(8,128)}) custom-call(s32[2]{0:T(128)} %pad_add_fusion.len_ref, bf16[1024,768]{1,0:T(8,128)(2,1)} %fusion.40.q_ref, bf16[2048,1536]{1,0:T(8,128)(2,1)} %add_convert_fusion.k_ref.v_ref, bf16[2048,1536]{1,0:T(8,128)(2,1)} %add_convert_fusion.k_ref.v_ref), custom_call_target="tpu_custom_call" | custom-call | flops 25769803776 | bytes 10000000 | tf_op jit(solution)/shard_map/attn_fwd/pallas_call | solution.py:70
  212.8 3.4 fusion.68
  217.7 34.5 %fusion.2 = (bf16[1024,3072]{1,0:T(8,128)(2,1)S(1)}, f32[1024,3072]{1,0:T(8,128)}) fusion(f32[3072]{0:T(1024)S(1)} %pad_maximum_fusion.9, bf16[768,6912]{1,0:T(8,128)(2,1)S(1)} %bitcast.93, f32[1024,768]{1,0:T(8,128)S(1)} %get-tuple-element.127, f32[768]{0:T(1024)S(1)} %copy-done.27, f32[768]{0:T(1024)S(1)} %copy-done.23, f32[1024]{0:T(1024)S(1)} %add_rsqrt_fusion.1, ...), kind=kOutput, calls=%fused_computation.4 | convolution fusion | flops 5043388416 | bytes 26767360 | tf_op jit(solution)/shard_map/dot_general | solution.py:196
  252.3 5.4 fusion.69
  258.3 1.2 fusion.29
  259.6 2.3 fusion.60
  261.9 6.9 %convolution_convert_fusion = bf16[768,3072]{1,0:T(8,128)(2,1)} fusion(bf16[1024,3072]{1,0:T(8,128)(2,1)S(1)} %bitcast.95, f32[1024,768]{1,0:T(8,128)S(1)} %get-tuple-element.89), kind=kOutput, calls=%fused_computation.30 | convolution fusion | flops 4834983936 | bytes 14155776 | tf_op jit(solution)/shard_map/dot_general | solution.py:192
  268.8 13.4 %convert_reduce_fusion = (f32[3072]{0:T(1024)}, bf16[1024,3072]{1,0:T(8,128)(2,1)S(1)}) fusion(f32[1024,3072]{1,0:T(8,128)} %get-tuple-element.129, f32[3072]{0:T(1024)S(1)} %pad_maximum_fusion.9, bf16[768,6912]{1,0:T(8,128)(2,1)S(1)} %bitcast.93, f32[1024,768]{1,0:T(8,128)S(1)} %get-tuple-element.89), kind=kOutput, calls=%fused_computation.11 | convolution fusion | flops 4873516032 | bytes 26763264 | tf_op jit(solution)/shard_map/dot_general | solution.py:196
  282.2 2.7 copy-done.30
  284.8 8.1 %convolution_convert_fusion.1 = bf16[768,3072]{1,0:T(8,128)(2,1)} fusion(bf16[1024,3072]{1,0:T(8,128)(2,1)S(1)} %get-tuple-element.134, f32[1024,768]{1,0:T(8,128)S(1)} %get-tuple-element.127, f32[768]{0:T(1024)S(1)} %copy-done.27, f32[768]{0:T(1024)S(1)} %copy-done.23, f32[1024]{0:T(1024)S(1)} %add_rsqrt_fusion.1, f32[1024]{0:T(1024)S(1)} %broadcast_multiply_fusion.5), kind=kOutput, calls=%fused_computation.31 | convolution fusion | flops 4838129664 | bytes 14170112 | tf_op jit(solution)/shard_map/dot_general | solution.py:192
  293.0 8.7 %multiply_reduce_fusion = (f32[768]{0:T(1024)}, f32[1024]{0:T(1024)S(1)}, f32[1024]{0:T(1024)S(1)}, f32[768]{0:T(1024)S(1)}, f32[1024,768]{1,0:T(8,128)S(1)}) fusion(f32[1024,768]{1,0:T(8,128)S(1)} %get-tuple-element.127, f32[1024]{0:T(1024)S(1)} %add_rsqrt_fusion.1, f32[1024]{0:T(1024)S(1)} %broadcast_multiply_fusion.5, f32[768]{0:T(1024)S(1)} %copy-done.23, ...), kind=kOutput, calls=%fused_computation.55 | convolution fusion | flops 4839698432 | bytes 20473856 | tf_op jit(solution)/shard_map/dot_general | solution.py:18
  303.1 2.5 convolution_convert_fusion.6
  305.6 2.4 copy.45
  308.0 9.2 %pad_maximum_fusion = bf16[768,6912]{1,0:T(8,128)(2,1)} fusion(bf16[768,3072]{1,0:T(8,128)(2,1)} %convolution_convert_fusion, bf16[768,3072]{1,0:T(8,128)(2,1)} %convolution_convert_fusion.1, bf16[768,768]{1,0:T(8,128)(2,1)} %copy.45), kind=kLoop, calls=%fused_computation.28 | loop fusion | flops 31850496 | bytes 21233664 | tf_op jit(solution)/shard_map/concatenate | solution.py:459
  317.1 3.8 convolution_convert_fusion.2.g_ref
  320.9 76.2 %attn_bwd.1 = (bf16[1024,768]{1,0:T(8,128)(2,1)}, bf16[2048,768]{1,0:T(8,128)(2,1)}, bf16[2048,768]{1,0:T(8,128)(2,1)}) custom-call(s32[2]{0:T(128)} %pad_add_fusion.len_ref, bf16[1024,768]{1,0:T(8,128)(2,1)} %fusion.40.q_ref, bf16[2048,1536]{1,0:T(8,128)(2,1)} %add_convert_fusion.k_ref.v_ref, bf16[2048,1536]{1,0:T(8,128)(2,1)} %add_convert_fusion.k_ref.v_ref, ...), custom_call_target="tpu_custom_call" | custom-call | flops 64424509440 | bytes 20000000 | tf_op jit(solution)/shard_map/attn_bwd/pallas_call | solution.py:170
  397.2 4.7 convolution_convert_fusion.3
  401.9 2.7 convolution_convert_fusion.4
  404.6 1.4 fusion.41
  406.4 4.1 copy.55
  411.1 24.9 %all-to-all-start = ((bf16[16,64,768]{2,1,0:T(8,128)(2,1)}), bf16[16,64,768]{2,1,0:T(8,128)(2,1)S(1)}, u32[]{:S(2)}, u32[]{:S(2)}) async-start(bf16[16,64,768]{2,1,0:T(8,128)(2,1)} %bitcast.9), calls=%async_computation | async-start | bytes 3145728 | tf_op jit(solution)/shard_map/all_to_all | solution.py:443
  436.5 2.8 convert_reduce_fusion.1
  439.3 4.8 fusion.43
  444.1 2.8 convolution_add_fusion
  447.0 3.1 slice_add_fusion
  450.1 1.3 slice.333
  452.0 85.1 %settle.1 = (bf16[16,64,768]{2,1,0:T(8,128)(2,1)}, f32[16,8,128]{2,1,0:T(8,128)}) custom-call(f32[16,64,768]{2,1,0:T(8,128)} %bitcast.79, bf16[16,64,768]{2,1,0:T(8,128)(2,1)} %bitcast.84, f32[16,8,128]{2,1,0:T(8,128)} %pad_bitcast_fusion.terms_ref), custom_call_target="tpu_custom_call" | custom-call | tf_op jit(solution)/shard_map/settle/pallas_call | solution.py:411
  539.9 1.3 copy.56
  542.6 1.9 collective-permute-start.3
  544.5 110.2 %reduce-scatter.5.cloned.1.call-done = bf16[48,6912]{1,0:T(8,128)(2,1)} async-done(((bf16[768,6912]{1,0:T(8,128)(2,1)}), bf16[48,6912]{1,0:T(8,128)(2,1)}) %reduce-scatter.5.cloned.1.call-update) | async-done | bytes 663568 | tf_op jit(solution)/shard_map/reduce_scatter | solution.py:464
  655.5 1.3 fusion.65
  657.7 1.5 collective-permute-start.4
  661.4 12.8 %collective-permute-done.4 = f32[48,3456]{1,0:T(8,128)} collective-permute-done((f32[48,3456]{1,0:T(8,128)}, f32[48,3456]{1,0:T(8,128)}, u32[]{:S(2)}, u32[]{:S(2)}) %collective-permute-start.4) | collective-permute-done | bytes 663584 | tf_op jit(solution)/shard_map/ppermute | solution.py:447
  674.3 1.2 select_add_fusion
  677.0 1.1 copy.81
  678.1 1.1 copy.82
  (169 shorter events, 23.1 us)
Async XLA Ops:
  7.2 20.2 %copy-start.8 = (f32[48,1536]{1,0:T(8,128)S(1)}, f32[48,1536]{1,0:T(8,128)}, u32[]{:S(2)}) copy-start(f32[48,1536]{1,0:T(8,128)} %param.23) | copy-start | bytes 884740
  7.2 20.1 %copy-start.7 = (f32[48,1536]{1,0:T(8,128)S(1)}, f32[48,1536]{1,0:T(8,128)}, u32[]{:S(2)}) copy-start(f32[48,1536]{1,0:T(8,128)} %param.22) | copy-start | bytes 884740
  7.2 20.1 %copy-start.13 = (f32[48,384]{1,0:T(8,128)S(1)}, f32[48,384]{1,0:T(8,128)}, u32[]{:S(2)}) copy-start(f32[48,384]{1,0:T(8,128)} %param.21) | copy-start | bytes 221188
  7.2 144.5 %all-gather.3.cloned.1.call-start = ((), (), s32[]{:S(2)}) async-start(), calls=%async_computation.4 | async-start | bytes 3760128 | tf_op jit(solution)/shard_map/all_gather | solution.py:495
  8.3 6.1 collective-permute-start
  15.3 197.5 %all-gather.5.cloned.1.call-start = ((), (), s32[]{:S(2)}) async-start(), calls=%async_computation.5 | async-start | bytes 11280384 | tf_op jit(solution)/shard_map/all_gather | solution.py:498
  18.2 9.0 %collective-permute-start.2 = (bf16[48,3456]{1,0:T(8,128)(2,1)S(1)}, bf16[48,3456]{1,0:T(8,128)(2,1)S(1)}, u32[]{:S(2)}, u32[]{:S(2)}) collective-permute-start(bf16[48,3456]{1,0:T(8,128)(2,1)S(1)} %pad_maximum_fusion.4), channel_id=1, source_target_pairs={{0,1},{1,0},{2,3},{3,2},{4,5},{5,4},{6,7},{7,6},{8,9},{9,8},{10,11... | collective-permute-start | bytes 995336 | tf_op jit(solution)/shard_map/ppermute | solution.py:447
  28.3 79.7 %copy-start.20 = (f32[2,384]{1,0:T(2,128)S(1)}, f32[2,384]{1,0:T(2,128)}, u32[]{:S(2)}) copy-start(f32[2,384]{1,0:T(2,128)} %param.24) | copy-start | bytes 9220
  28.3 79.7 %copy-start.18 = (f32[1536]{0:T(1024)S(1)}, f32[1536]{0:T(1024)}, u32[]{:S(2)}) copy-start(f32[1536]{0:T(1024)} %param.26) | copy-start | bytes 18436
  28.4 80.4 %copy-start.28 = (s32[16]{0:T(128)S(1)}, s32[16]{0:T(128)}, u32[]{:S(2)}) copy-start(s32[16]{0:T(128)} %param.19) | copy-start | bytes 196
  28.4 83.0 %copy-start.29 = (s32[16]{0:T(128)S(1)}, s32[16]{0:T(128)}, u32[]{:S(2)}) copy-start(s32[16]{0:T(128)} %param.18) | copy-start | bytes 196
  83.8 66.5 %copy-start.17 = (f32[768]{0:T(1024)S(1)}, f32[768]{0:T(1024)}, u32[]{:S(2)}) copy-start(f32[768]{0:T(1024)} %param.30) | copy-start | bytes 9220
  83.8 66.5 %all-to-all-start.1 = ((bf16[16,64,768]{2,1,0:T(8,128)(2,1)}), bf16[16,64,768]{2,1,0:T(8,128)(2,1)S(1)}, u32[]{:S(2)}, u32[]{:S(2)}) async-start(bf16[16,64,768]{2,1,0:T(8,128)(2,1)} %bitcast.11), calls=%async_computation.1 | async-start | bytes 3145728 | tf_op jit(solution)/shard_map/all_to_all | solution.py:437
  108.0 431.9 %reduce-scatter.7.cloned.1.call-start = ((), (), s32[]{:S(2)}) async-start(), calls=%async_computation.7 | async-start | bytes 3760128
  108.1 6.6 collective-permute-start.1
  114.7 98.1 %copy-start.9 = (bf16[1,16,64,768]{3,2,1,0:T(8,128)(2,1)}, bf16[1,16,64,768]{3,2,1,0:T(8,128)(2,1)S(1)}, u32[]{:S(2)}) copy-start(bf16[1,16,64,768]{3,2,1,0:T(8,128)(2,1)S(1)} %slice.173) | copy-start | bytes 4718596
  151.7 4.0 copy-start.2
  151.7 4.0 copy-start.14
  162.8 50.0 %copy-start.25 = (f32[768]{0:T(1024)S(1)}, f32[768]{0:T(1024)}, u32[]{:S(2)}) copy-start(f32[768]{0:T(1024)} %param.25) | copy-start | bytes 9220
  212.8 4.1 slice-start
  212.8 4.3 slice-start.1
  212.8 4.9 slice-start.2
  216.3 1.4 copy-start.23
  216.3 1.4 copy-start.27
  217.7 34.5 %copy-start.26 = (f32[768]{0:T(1024)S(1)}, f32[768]{0:T(1024)}, u32[]{:S(2)}) copy-start(f32[768]{0:T(1024)} %param.27) | copy-start | bytes 9220
  252.3 5.5 copy-start.31
  258.3 1.3 copy-start.22
  258.3 3.6 slice-start.3
  259.6 2.3 slice-start.4
  282.2 2.7 copy-start.30
  301.7 1.4 copy-start.33
  302.8 14.4 %copy-start = (f32[1024,768]{1,0:T(8,128)}, f32[1024,768]{1,0:T(8,128)S(1)}, u32[]{:S(2)}) copy-start(f32[1024,768]{1,0:T(8,128)S(1)} %get-tuple-element.91) | copy-start | bytes 9437188
  320.9 76.2 %copy-start.3 = (bf16[2,16,64,768]{3,2,1,0:T(8,128)(2,1)S(1)}, bf16[2,16,64,768]{3,2,1,0:T(8,128)(2,1)}, u32[]{:S(2)}) copy-start(bf16[2,16,64,768]{3,2,1,0:T(8,128)(2,1)} %deal_both.1) | copy-start | bytes 9437188
  397.2 4.7 copy-start.32
  401.9 2.7 copy-start.4
  401.9 2.7 copy-start.10
  410.5 244.2 %reduce-scatter.5.cloned.1.call-start = ((), (), s32[]{:S(2)}) async-start(), calls=%async_computation.6 | async-start | bytes 11280384 | tf_op jit(solution)/shard_map/reduce_scatter | solution.py:464
  411.1 25.0 %copy-start.24 = (f32[768]{0:T(1024)S(1)}, f32[768]{0:T(1024)}, u32[]{:S(2)}) copy-start(f32[768]{0:T(1024)} %get-tuple-element.78) | copy-start | bytes 9220
  411.1 25.1 %copy-start.19 = (f32[768]{0:T(1024)S(1)}, f32[768]{0:T(1024)}, u32[]{:S(2)}) copy-start(f32[768]{0:T(1024)} %get-tuple-element.84) | copy-start | bytes 9220
  411.1 25.1 %copy-start.5 = (bf16[1024,768]{1,0:T(8,128)(2,1)S(1)}, bf16[1024,768]{1,0:T(8,128)(2,1)}, u32[]{:S(2)}) copy-start(bf16[1024,768]{1,0:T(8,128)(2,1)} %get-tuple-element.30) | copy-start | bytes 4718596
  411.1 248.6 %all-to-all-start = ((bf16[16,64,768]{2,1,0:T(8,128)(2,1)}), bf16[16,64,768]{2,1,0:T(8,128)(2,1)S(1)}, u32[]{:S(2)}, u32[]{:S(2)}) async-start(bf16[16,64,768]{2,1,0:T(8,128)(2,1)} %bitcast.9), calls=%async_computation | async-start | bytes 3145728 | tf_op jit(solution)/shard_map/all_to_all | solution.py:443
  436.1 3.2 copy-start.15
  439.3 4.9 copy-start.6
  444.1 2.8 copy-start.1
  450.1 1.3 copy-start.21
  542.6 117.1 %collective-permute-start.3 = (f32[48,1152]{1,0:T(8,128)}, f32[48,1152]{1,0:T(8,128)}, u32[]{:S(2)}, u32[]{:S(2)}) collective-permute-start(f32[48,1152]{1,0:T(8,128)} %fusion.57), channel_id=1, source_target_pairs={{0,1},{1,0},{2,3},{3,2},{4,5},{5,4},{6,7},{7,6},{8,9},{9,8},{10,11... | collective-permute-start | bytes 663560 | tf_op jit(solution)/shard_map/ppermute | solution.py:447
  657.7 16.6 %collective-permute-start.4 = (f32[48,3456]{1,0:T(8,128)}, f32[48,3456]{1,0:T(8,128)}, u32[]{:S(2)}, u32[]{:S(2)}) collective-permute-start(f32[48,3456]{1,0:T(8,128)} %fusion.56), channel_id=1, source_target_pairs={{0,1},{1,0},{2,3},{3,2},{4,5},{5,4},{6,7},{7,6},{8,9},{9,8},{10,11... | collective-permute-start | bytes 1990664 | tf_op jit(solution)/shard_map/ppermute | solution.py:447
  661.4 16.7 %copy-start.11 = (bf16[16,64,768]{2,1,0:T(8,128)(2,1)S(1)}, bf16[16,64,768]{2,1,0:T(8,128)(2,1)}, u32[]{:S(2)}) copy-start(bf16[16,64,768]{2,1,0:T(8,128)(2,1)} %get-tuple-element.33) | copy-start | bytes 4718596
  (2 other events, 1.5 us)
Sparse Core Ops, SparseCore 0:
  15.4 69.3 all-gather.2
  87.1 113.2 all-gather.4
  410.6 118.7 reduce-scatter.6
  533.3 121.3 reduce-scatter.4
